TPU v7x, 128 devices: a whole 4x4x4 slice. The times are simulated.
128 devices in a mesh: data: 1, outer: 16 (over z, y), expert: 8 (over x, core).
Axes of the slice: x: 4, y: 4, z: 4, core: 2. Of those that a mesh axis runs over, the one named last changes fastest.
Arguments:
- x: bfloat16 [32768, 2048], P(('data', 'outer', 'expert'))
- wr: bfloat16 [2048, 128], replicated
- idx: int32 [32768, 8], P(('data', 'outer', 'expert'))
- w1: bfloat16 [128, 2048, 768], P(('outer', 'expert'))
- w3: bfloat16 [128, 2048, 768], P(('outer', 'expert'))
- w2: bfloat16 [128, 768, 2048], P(('outer', 'expert'))
Outputs:
- output: bfloat16 [32768, 2048], P(('data', 'outer', 'expert'))
All inputs are finite; a program needn't handle non-finite values.
Results may differ from a plain program's by a relative error of at most 0.00816633.
Values are sent between devices in bfloat16 or wider.
A program may use at most 1 GiB of HBM per device.

v0:
```python
import jax
import jax.numpy as jnp
from jax import lax
from jax.sharding import PartitionSpec as P


def _gate(x, wr, idx):
    logits = jnp.dot(x, wr, preferred_element_type=jnp.float32)
    oh = idx[:, :, None] == jnp.arange(wr.shape[1], dtype=idx.dtype)
    return jax.nn.softmax(jnp.sum(jnp.where(oh, logits[:, None, :], 0.0), axis=-1), axis=-1)


def _plan(idx, g, base, ne, cap):
    t = idx.shape[-2]
    oh = idx[..., None] == base + jnp.arange(ne, dtype=idx.dtype)
    m = jnp.sum(oh, axis=-2, dtype=jnp.int32).astype(jnp.float32)
    pos = jnp.arange(t, dtype=jnp.int32)
    tri = (pos[None, :] < pos[:, None]).astype(jnp.bfloat16)
    cnt = jnp.einsum('uv,...ve->...ue', tri, m.astype(jnp.bfloat16), preferred_element_type=jnp.float32)
    c = jnp.arange(cap, dtype=jnp.float32)
    hit = (c >= cnt[..., None]) & (c < (cnt + m)[..., None])
    ge = jnp.sum(jnp.where(oh, g[..., None], 0.0), axis=-2)
    w = jnp.where(hit, ge[..., None], 0.0)
    return hit.astype(jnp.bfloat16), w


def _split(w):
    hi = w.astype(jnp.bfloat16)
    r = w - hi.astype(jnp.float32)
    mid = r.astype(jnp.bfloat16)
    lo = (r - mid.astype(jnp.float32)).astype(jnp.bfloat16)
    return jnp.stack([hi, mid, lo])


def solution(mesh):
    O = mesh.shape['outer']
    X = mesh.shape['expert']
    n = O * X
    tok = P(('data', 'outer', 'expert'), None)
    wsp = P(('outer', 'expert'), None, None)

    def local(x, wr, idx, w1, w3, w2):
        T, dm = x.shape
        k = idx.shape[1]
        E = wr.shape[1]
        el = w1.shape[0]
        C = 2 * T * k // E
        g = _gate(x, wr, idx)
        hit, w = _plan(idx, g, 0, E, C)
        ws = _split(w).reshape(3 * T, E * C)
        buf = jnp.einsum('tec,td->ecd', hit, x, preferred_element_type=jnp.float32).astype(x.dtype)
        buf = buf.reshape(O, X, el * C, dm)
        buf = lax.all_to_all(buf, 'expert', 1, 1, tiled=True)
        buf = lax.all_to_all(buf, 'outer', 0, 0, tiled=True)
        xin = buf.reshape(n, el, C, dm).transpose(1, 0, 2, 3).reshape(el, n * C, dm)
        a = jnp.einsum('ecd,edf->ecf', xin, w1, preferred_element_type=jnp.float32)
        b = jnp.einsum('ecd,edf->ecf', xin, w3, preferred_element_type=jnp.float32)
        h = (jax.nn.silu(a) * b).astype(jnp.bfloat16)
        o = jnp.einsum('ecf,efd->ecd', h, w2, preferred_element_type=jnp.float32).astype(jnp.bfloat16)
        o = o.reshape(el, n, C, dm).transpose(1, 0, 2, 3).reshape(O, X, el * C, dm)
        o = lax.all_to_all(o, 'outer', 0, 0, tiled=True)
        o = lax.all_to_all(o, 'expert', 1, 1, tiled=True)
        y = jnp.dot(ws, o.reshape(E * C, dm), preferred_element_type=jnp.float32)
        return jnp.sum(y.reshape(3, T, dm), axis=0).astype(jnp.bfloat16)

    return jax.shard_map(local, mesh=mesh, in_specs=(tok, P(None, None), tok, wsp, wsp, wsp), out_specs=tok, check_vma=False)
```

profile of v0, /device:TPU:0, one launch (start us, length us, event | category | flops | bytes accessed | tf_op | source)
XLA Modules:
  0.0 931.2 jit_solution(5348263969141501188)
XLA Ops:
  0.0 0.0 copy-start
  0.0 1.0 copy.58
  1.0 0.0 copy-start.4
  1.0 0.4 convert_reduce_fusion
  1.4 0.8 convert_add_fusion
  2.2 0.1 copy.61
  2.3 0.0 copy-start.11
  2.3 1.0 copy.59
  3.4 0.0 copy-start.9
  3.4 1.8 fusion.6
  5.2 11.8 %convert_bitcast_fusion = bf16[16,8,32,2048]{3,1,0,2:T(8,128)(2,1)} fusion(pred[256,128,32]{0,2,1:T(32,128)(4,1)} %fusion.6, bf16[256,2048]{1,0:T(8,128)(2,1)} %param.6), kind=kOutput, calls=%fused_computation | convolution fusion | flops 4303355904 | bytes 18874368 | tf_op jit(solution)/shard_map/tec,td->ecd/dot_general | solution.py:51
  17.0 0.0 copy-done.4
  17.0 0.0 copy-done.11
  17.0 0.0 copy-done.9
  17.0 15.1 %copy.69 = bf16[16,8,32,2048]{3,2,0,1:T(8,128)(2,1)S(1)} copy(bf16[16,8,32,2048]{3,1,0,2:T(8,128)(2,1)} %convert_bitcast_fusion) | data formatting | bytes 33554432 | tf_op jit(solution)/shard_map/reshape | solution.py:52
  32.2 188.8 %all_to_all.20 = bf16[16,8,32,2048]{3,2,0,1:T(8,128)(2,1)S(1)} all-to-all(bf16[16,8,32,2048]{3,2,0,1:T(8,128)(2,1)S(1)} %copy.69), channel_id=1, replica_groups=mesh['data'=1,'outer'=16,'expert'=8] {'expert'}, dimensions={1} | all-to-all | bytes 33554432 | tf_op jit(solution)/shard_map/all_to_all | solution.py:53
  221.0 2.2 copy.70
  223.2 0.0 copy-start.14
  223.2 198.5 %all_to_all.21 = bf16[16,8,32,2048]{3,2,1,0:T(8,128)(2,1)S(1)} all-to-all(bf16[16,8,32,2048]{3,2,1,0:T(8,128)(2,1)S(1)} %copy.70), channel_id=1, replica_groups=mesh['data'=1,'outer'=16,'expert'=8] {'outer'}, dimensions={0} | all-to-all | bytes 33554432 | tf_op jit(solution)/shard_map/all_to_all | solution.py:54
  421.7 0.0 copy-start.2
  421.7 5.7 copy-done.2
  427.4 0.0 copy-done.14
  427.4 16.6 %fusion.11 = f32[4096,768]{1,0:T(8,128)} fusion(bf16[4096,2048]{1,0:T(8,128)(2,1)S(1)} %bitcast.29, bf16[1,2048,768]{2,1,0:T(8,128)(2,1)S(1)} %copy-done.14), kind=kOutput, calls=%fused_computation.18 | convolution fusion | flops 12884901888 | bytes 32505856 | tf_op jit(solution)/shard_map/ecd,edf->ecf/dot_general | solution.py:56
  444.0 0.0 copy-done
  444.0 36.5 %convolution_convert_fusion = bf16[4096,2048]{1,0:T(8,128)(2,1)} fusion(f32[4096,768]{1,0:T(8,128)} %fusion.11, bf16[4096,2048]{1,0:T(8,128)(2,1)} %bitcast.30, bf16[1,768,2048]{2,1,0:T(8,128)(2,1)S(1)} %copy-done, bf16[1,2048,768]{2,1,0:T(8,128)(2,1)} %param.10), kind=kOutput, calls=%fused_computation.1 | convolution fusion | flops 25797066752 | bytes 52428800 | tf_op jit(solution)/shard_map/ecf,efd->ecd/dot_general | solution.py:59
  480.4 217.4 %all_to_all.22 = bf16[16,8,32,2048]{3,2,1,0:T(8,128)(2,1)S(1)} all-to-all(bf16[16,8,32,2048]{3,2,1,0:T(8,128)(2,1)} %bitcast.31), channel_id=1, replica_groups=mesh['data'=1,'outer'=16,'expert'=8] {'outer'}, dimensions={0} | all-to-all | bytes 33554432 | tf_op jit(solution)/shard_map/all_to_all | solution.py:61
  697.9 6.5 copy.71
  704.4 0.0 copy-start.3
  704.4 0.0 copy-start.13
  704.4 0.0 copy-start.5
  704.4 9.0 all-to-all-start.3
  713.4 0.0 copy-done.3
  713.4 0.0 copy-done.13
  713.4 0.4 fusion.24
  713.9 0.0 copy-done.5
  713.9 0.9 select_reduce_fusion.1
  714.8 0.1 copy.64
  714.8 0.1 reduce_max.9
  715.0 0.1 copy.65
  715.1 1.3 select_reduce_fusion
  716.4 0.1 copy.66
  716.5 2.3 broadcast_in_dim.54
  718.8 0.0 copy-start.12
  718.8 5.7 copy.67
  724.5 0.0 copy-done.12
  724.5 2.2 lt.49
  726.7 0.0 copy-start.10
  726.7 5.7 copy.62
  732.4 0.0 copy-done.10
  732.4 2.3 ge.52
  734.7 5.6 copy.60
  740.3 0.1 ge.50
  740.4 7.2 fusion.23
  747.6 2.8 fusion.13
  750.4 147.6 %all-to-all-done.3 = bf16[16,8,32,2048]{3,2,0,1:T(8,128)(2,1)} async-done(((bf16[16,8,32,2048]{3,2,0,1:T(8,128)(2,1)}), bf16[16,8,32,2048]{3,2,0,1:T(8,128)(2,1)}, u32[]{:S(2)}, u32[]{:S(2)}) %all-to-all-start.3) | async-done | bytes 16777248 | tf_op jit(solution)/shard_map/all_to_all | solution.py:62
  898.0 0.0 copy-start.6
  898.0 0.0 copy-start.7
  898.0 15.1 %copy.72 = bf16[16,8,32,2048]{3,2,1,0:T(8,128)(2,1)} copy(bf16[16,8,32,2048]{3,2,0,1:T(8,128)(2,1)} %all-to-all-done.3) | data formatting | bytes 33554432 | tf_op jit(solution)/shard_map/all_to_all | solution.py:62
  913.1 0.0 copy-done.6
  913.1 0.0 copy-done.7
  913.1 0.0 copy-done.8
  913.1 0.0 copy-start.1
  913.1 18.1 %fusion.14 = bf16[256,2048]{1,0:T(8,128)(2,1)} fusion(bf16[4096,2048,1]{1,0,2:T(8,128)(2,1)} %bitcast.28, bf16[1,256,4096]{2,1,0:T(8,128)(2,1)S(1)} %copy-done.7, bf16[1,256,4096]{2,1,0:T(8,128)(2,1)S(1)} %copy-done.6, bf16[1,256,4096]{2,1,0:T(8,128)(2,1)S(1)} %copy-done.8), kind=kOutput, calls=%fused_computation.21 | convolution fusion | flops 12892241920 | bytes 24117248 | tf_op jit(solution)/shard_map/dot_general | solution.py:63
  931.2 0.0 copy-done.1
  (4 shorter events, 0.1 us)
Async XLA Ops:
  0.0 444.0 %copy-start = (bf16[1,768,2048]{2,1,0:T(8,128)(2,1)S(1)}, bf16[1,768,2048]{2,1,0:T(8,128)(2,1)}, u32[]{:S(2)}) copy-start(bf16[1,768,2048]{2,1,0:T(8,128)(2,1)} %param.11) | copy-start | bytes 9437188
  1.0 16.0 %copy-start.4 = (s32[256,8]{1,0:T(8,128)}, s32[256,8]{1,0:T(8,128)S(1)}, u32[]{:S(2)}) copy-start(s32[256,8]{1,0:T(8,128)S(1)} %copy.58) | copy-start | bytes 24580
  2.3 14.7 %copy-start.11 = (f32[256,128]{0,1:T(8,128)}, f32[256,128]{0,1:T(8,128)S(1)}, u32[]{:S(2)}) copy-start(f32[256,128]{0,1:T(8,128)S(1)} %copy.61) | copy-start | bytes 393220
  3.4 13.6 %copy-start.9 = (f32[256,128]{0,1:T(8,128)}, f32[256,128]{0,1:T(8,128)S(1)}, u32[]{:S(2)}) copy-start(f32[256,128]{0,1:T(8,128)S(1)} %copy.59) | copy-start | bytes 393220
  223.2 204.2 %copy-start.14 = (bf16[1,2048,768]{2,1,0:T(8,128)(2,1)S(1)}, bf16[1,2048,768]{2,1,0:T(8,128)(2,1)}, u32[]{:S(2)}) copy-start(bf16[1,2048,768]{2,1,0:T(8,128)(2,1)} %param.9) | copy-start | bytes 9437188
  421.7 5.7 copy-start.2
  704.4 9.0 copy-start.3
  704.4 9.0 copy-start.13
  704.4 9.5 %copy-start.5 = (s32[256,8]{1,0:T(8,128)S(1)}, s32[256,8]{1,0:T(8,128)}, u32[]{:S(2)}) copy-start(s32[256,8]{1,0:T(8,128)} %copy-done.4) | copy-start | bytes 24580
  704.4 193.6 %all-to-all-start.3 = ((bf16[16,8,32,2048]{3,2,0,1:T(8,128)(2,1)}), bf16[16,8,32,2048]{3,2,0,1:T(8,128)(2,1)}, u32[]{:S(2)}, u32[]{:S(2)}) async-start(bf16[16,8,32,2048]{3,2,0,1:T(8,128)(2,1)} %copy.71), calls=%async_computation.3 | async-start | bytes 33554432 | tf_op jit(solution)/shard_map/all_to_all | solution.py:62
  718.8 5.7 copy-start.12
  726.7 5.7 copy-start.10
  898.0 15.1 %copy-start.6 = (bf16[1,256,4096]{2,1,0:T(8,128)(2,1)S(1)}, bf16[1,256,4096]{2,1,0:T(8,128)(2,1)}, u32[]{:S(2)}) copy-start(bf16[1,256,4096]{2,1,0:T(8,128)(2,1)} %get-tuple-element.7) | copy-start | bytes 6291460
  898.0 15.1 %copy-start.7 = (bf16[1,256,4096]{2,1,0:T(8,128)(2,1)S(1)}, bf16[1,256,4096]{2,1,0:T(8,128)(2,1)}, u32[]{:S(2)}) copy-start(bf16[1,256,4096]{2,1,0:T(8,128)(2,1)} %get-tuple-element.8) | copy-start | bytes 6291460
  898.0 15.1 %copy-start.8 = (bf16[1,256,4096]{2,1,0:T(8,128)(2,1)S(1)}, bf16[1,256,4096]{2,1,0:T(8,128)(2,1)}, u32[]{:S(2)}) copy-start(bf16[1,256,4096]{2,1,0:T(8,128)(2,1)} %get-tuple-element.5) | copy-start | bytes 6291460
  913.1 18.1 %copy-start.1 = (bf16[1,768,2048]{2,1,0:T(8,128)(2,1)S(1)}, bf16[1,768,2048]{2,1,0:T(8,128)(2,1)}, u32[]{:S(2)}) copy-start(bf16[1,768,2048]{2,1,0:T(8,128)(2,1)} %param.11) | copy-start | bytes 9437188
where the time goes:
time: 932 us; the launch traced here: 931 us
  blocking collectives  605 us (65%)
  waiting for transfers between devices  148 us (16%)
  matrix products  84.2 us (9%)
  local copies, waits for them, and re-layouts  71 us (8%)
  other arithmetic  14.4 us (2%)
    all_to_all x1, blocking collectives, local(): o = lax.all_to_all(o, 'outer', 0, 0, tiled=True)  217 us
    all_to_all x1, blocking collectives, local(): buf = lax.all_to_all(buf, 'outer', 0, 0, tiled=True)  198 us
    all_to_all x1, blocking collectives, local(): buf = lax.all_to_all(buf, 'expert', 1, 1, tiled=True)  189 us
    all_to_all x1, waiting for transfers between devices, local(): o = lax.all_to_all(o, 'expert', 1, 1, tiled=True)  148 us
    dot_general x1, matrix products, local(): jnp.einsum('ecf,efd->ecd', h, w2, preferred_element_type=jnp.float32)  36.5 us
  transfers between devices with their start and end apart: 1, of which 1 were waited for; matrix products, arithmetic and copies ran while one was open for 4% of the time, Pallas kernels for 0%

commit v1 on v0

--- a/solution.py
+++ b/solution.py
@@ -49,17 +49,15 @@
         hit, w = _plan(idx, g, 0, E, C)
         ws = _split(w).reshape(3 * T, E * C)
         buf = jnp.einsum('tec,td->ecd', hit, x, preferred_element_type=jnp.float32).astype(x.dtype)
-        buf = buf.reshape(O, X, el * C, dm)
-        buf = lax.all_to_all(buf, 'expert', 1, 1, tiled=True)
-        buf = lax.all_to_all(buf, 'outer', 0, 0, tiled=True)
+        buf = buf.reshape(n, el * C, dm)
+        buf = lax.all_to_all(buf, ('outer', 'expert'), 0, 0, tiled=True)
         xin = buf.reshape(n, el, C, dm).transpose(1, 0, 2, 3).reshape(el, n * C, dm)
         a = jnp.einsum('ecd,edf->ecf', xin, w1, preferred_element_type=jnp.float32)
         b = jnp.einsum('ecd,edf->ecf', xin, w3, preferred_element_type=jnp.float32)
         h = (jax.nn.silu(a) * b).astype(jnp.bfloat16)
         o = jnp.einsum('ecf,efd->ecd', h, w2, preferred_element_type=jnp.float32).astype(jnp.bfloat16)
-        o = o.reshape(el, n, C, dm).transpose(1, 0, 2, 3).reshape(O, X, el * C, dm)
-        o = lax.all_to_all(o, 'outer', 0, 0, tiled=True)
-        o = lax.all_to_all(o, 'expert', 1, 1, tiled=True)
+        o = o.reshape(el, n, C, dm).transpose(1, 0, 2, 3).reshape(n, el * C, dm)
+        o = lax.all_to_all(o, ('outer', 'expert'), 0, 0, tiled=True)
         y = jnp.dot(ws, o.reshape(E * C, dm), preferred_element_type=jnp.float32)
         return jnp.sum(y.reshape(3, T, dm), axis=0).astype(jnp.bfloat16)
 

time: 932 us -> 609 us (0.65)
  the two profiles are of different devices: /device:TPU:0 before, /device:TPU:2 now
where the time goes in v1:
time: 609 us
  waiting for transfers between devices  241 us (40%)
  blocking collectives  224 us (37%)
  matrix products  97.2 us (16%)
  local copies, waits for them, and re-layouts  23.5 us (4%)
  starting transfers between devices  14.8 us (2%)
  other arithmetic  7.91 us (1%)
    all_to_all x1, waiting for transfers between devices, local(): o = lax.all_to_all(o, ('outer', 'expert'), 0, 0, tiled=True)  241 us
    all_to_all x1, blocking collectives, local(): buf = lax.all_to_all(buf, ('outer', 'expert'), 0, 0, tiled=True)  224 us
    dot_general x1, matrix products, local(): jnp.einsum('ecf,efd->ecd', h, w2, preferred_element_type=jnp.float32)  36.5 us
    dot_general x1, matrix products, local(): y = jnp.dot(ws, o.reshape(E * C, dm), preferred_element_type=jnp.float32)  34.1 us
    dot_general x1, matrix products, local(): a = jnp.einsum('ecd,edf->ecf', xin, w1, preferred_element_type=jnp.float32)  16.6 us
    convert_element_type x1, local copies, waits for them, and re-layouts, local(): jnp.einsum('tec,td->ecd', hit, x, preferred_element_type=jnp.float32)  15.1 us
    all_to_all x1, starting transfers between devices, local(): o = lax.all_to_all(o, ('outer', 'expert'), 0, 0, tiled=True)  14.8 us
  transfers between devices with their start and end apart: 1, of which 1 were waited for; matrix products, arithmetic and copies ran while one was open for 1% of the time, Pallas kernels for 0%

profile of v1, /device:TPU:2, one launch (start us, length us, event | category | flops | bytes accessed | tf_op | source)
XLA Modules:
  0.0 608.7 jit_solution(6896693603659179678)
XLA Ops:
  0.0 0.0 copy-start
  0.0 1.0 copy.30
  1.0 0.4 convert_reduce_fusion
  1.4 0.2 convert_add_fusion
  1.6 0.8 copy.35
  2.3 0.7 copy.34
  3.1 9.4 %convolution_convert_fusion.1 = bf16[128,32,2048]{2,0,1:T(8,128)(2,1)} fusion(f32[256,128]{0,1:T(8,128)} %copy.35, f32[256,128]{0,1:T(8,128)} %copy.34, bf16[256,2048]{1,0:T(8,128)(2,1)} %param.6), kind=kOutput, calls=%fused_computation.4 | convolution fusion | flops 4306501632 | bytes 18087936 | tf_op jit(solution)/shard_map/tec,td->ecd/dot_general | solution.py:51
  12.5 15.1 %copy.36 = bf16[128,32,2048]{2,1,0:T(8,128)(2,1)S(1)} copy(bf16[128,32,2048]{2,0,1:T(8,128)(2,1)} %convolution_convert_fusion.1) | data formatting | bytes 33554432 | tf_op jit(solution)/shard_map/convert_element_type | solution.py:51
  27.6 0.0 copy-start.5
  27.6 224.0 %all_to_all.10 = bf16[128,32,2048]{2,1,0:T(8,128)(2,1)S(1)} all-to-all(bf16[128,32,2048]{2,1,0:T(8,128)(2,1)S(1)} %copy.36), channel_id=1, replica_groups=mesh['data'=1,'outer'=16,'expert'=8] {'outer','expert'}, dimensions={0} | all-to-all | bytes 33554432 | tf_op jit(solution)/shard_map/all_to_all | solution.py:53
  251.6 0.0 copy-start.2
  251.6 5.7 copy-done.2
  257.3 0.0 copy-done.5
  257.3 16.6 %fusion.19 = f32[4096,768]{1,0:T(8,128)} fusion(bf16[4096,2048]{1,0:T(8,128)(2,1)S(1)} %bitcast.28, bf16[1,2048,768]{2,1,0:T(8,128)(2,1)S(1)} %copy-done.5), kind=kOutput, calls=%fused_computation.24 | convolution fusion | flops 12884901888 | bytes 32505856 | tf_op jit(solution)/shard_map/ecd,edf->ecf/dot_general | solution.py:55
  273.9 0.0 copy-done
  273.9 36.5 %convolution_convert_fusion = bf16[4096,2048]{1,0:T(8,128)(2,1)} fusion(f32[4096,768]{1,0:T(8,128)} %fusion.19, bf16[4096,2048]{1,0:T(8,128)(2,1)} %bitcast.29, bf16[1,768,2048]{2,1,0:T(8,128)(2,1)S(1)} %copy-done, bf16[1,2048,768]{2,1,0:T(8,128)(2,1)} %param.10), kind=kOutput, calls=%fused_computation.3 | convolution fusion | flops 25797066752 | bytes 52428800 | tf_op jit(solution)/shard_map/ecf,efd->ecd/dot_general | solution.py:58
  310.4 0.0 copy-start.3
  310.4 0.0 copy-start.4
  310.4 14.8 %all-to-all-start.1 = ((bf16[128,32,2048]{2,1,0:T(8,128)(2,1)}), bf16[128,32,2048]{2,1,0:T(8,128)(2,1)}, u32[]{:S(2)}, u32[]{:S(2)}) async-start(bf16[128,32,2048]{2,1,0:T(8,128)(2,1)} %bitcast.27), calls=%async_computation.1 | async-start | bytes 33554432 | tf_op jit(solution)/shard_map/all_to_all | solution.py:60
  325.2 0.0 copy-done.3
  325.2 0.0 copy-done.4
  325.2 0.4 fusion.29
  325.6 0.9 select_reduce_fusion.1
  326.5 0.1 copy.32
  326.6 0.1 reduce_max.9
  326.8 0.1 copy.33
  326.9 1.3 select_reduce_fusion
  328.2 2.0 select_convert_fusion
  330.1 3.3 fusion.8
  333.4 241.2 %all-to-all-done.1 = bf16[128,32,2048]{2,1,0:T(8,128)(2,1)} async-done(((bf16[128,32,2048]{2,1,0:T(8,128)(2,1)}), bf16[128,32,2048]{2,1,0:T(8,128)(2,1)}, u32[]{:S(2)}, u32[]{:S(2)}) %all-to-all-start.1) | async-done | bytes 16777248 | tf_op jit(solution)/shard_map/all_to_all | solution.py:60
  574.6 0.0 copy-start.1
  574.6 34.1 %bitcast_reduce_fusion = bf16[256,2048]{1,0:T(8,128)(2,1)} fusion(bf16[128,32,2048]{2,1,0:T(8,128)(2,1)} %all-to-all-done.1, bf16[1,256,128,32]{2,1,3,0:T(8,128)(2,1)} %get-tuple-element.6, bf16[1,256,128,32]{2,1,3,0:T(8,128)(2,1)} %get-tuple-element.5, bf16[1,256,128,32]{2,1,3,0:T(8,128)(2,1)} %select_convert_fusion), kind=kOutput, calls=%fused_computation.11 | convolution fusion | flops 12892241920 | bytes 24117248 | tf_op jit(solution)/shard_map/dot_general | solution.py:61
  608.7 0.0 copy-done.1
  (2 shorter events, 0.0 us)
Async XLA Ops:
  0.0 273.9 %copy-start = (bf16[1,768,2048]{2,1,0:T(8,128)(2,1)S(1)}, bf16[1,768,2048]{2,1,0:T(8,128)(2,1)}, u32[]{:S(2)}) copy-start(bf16[1,768,2048]{2,1,0:T(8,128)(2,1)} %param.11) | copy-start | bytes 9437188
  27.6 229.7 %copy-start.5 = (bf16[1,2048,768]{2,1,0:T(8,128)(2,1)S(1)}, bf16[1,2048,768]{2,1,0:T(8,128)(2,1)}, u32[]{:S(2)}) copy-start(bf16[1,2048,768]{2,1,0:T(8,128)(2,1)} %param.9) | copy-start | bytes 9437188
  251.6 5.7 copy-start.2
  310.4 14.8 %copy-start.3 = (bf16[256,2048]{1,0:T(8,128)(2,1)S(1)}, bf16[256,2048]{1,0:T(8,128)(2,1)}, u32[]{:S(2)}) copy-start(bf16[256,2048]{1,0:T(8,128)(2,1)} %param.6) | copy-start | bytes 3145732
  310.4 14.8 %copy-start.4 = (bf16[2048,128]{1,0:T(8,128)(2,1)S(1)}, bf16[2048,128]{1,0:T(8,128)(2,1)}, u32[]{:S(2)}) copy-start(bf16[2048,128]{1,0:T(8,128)(2,1)} %param.7) | copy-start | bytes 1572868
  310.4 264.1 %all-to-all-start.1 = ((bf16[128,32,2048]{2,1,0:T(8,128)(2,1)}), bf16[128,32,2048]{2,1,0:T(8,128)(2,1)}, u32[]{:S(2)}, u32[]{:S(2)}) async-start(bf16[128,32,2048]{2,1,0:T(8,128)(2,1)} %bitcast.27), calls=%async_computation.1 | async-start | bytes 33554432 | tf_op jit(solution)/shard_map/all_to_all | solution.py:60
  574.6 34.1 %copy-start.1 = (bf16[1,768,2048]{2,1,0:T(8,128)(2,1)S(1)}, bf16[1,768,2048]{2,1,0:T(8,128)(2,1)}, u32[]{:S(2)}) copy-start(bf16[1,768,2048]{2,1,0:T(8,128)(2,1)} %param.11) | copy-start | bytes 9437188

commit v2 on v1

v2 whole, which is shorter than its diff:
```python
import functools

import jax
import jax.numpy as jnp
from jax import lax
from jax.experimental import pallas as pl
from jax.experimental.pallas import tpu as pltpu
from jax.sharding import PartitionSpec as P

MESH = pl.DeviceIdType.MESH
F32 = jnp.float32
BF16 = jnp.bfloat16


def _cols(d):
    t = d // 128
    w = [(t // 3) * 128, (t // 3) * 128, (t - 2 * (t // 3)) * 128]
    return [(0, w[0]), (w[0], w[1]), (w[0] + w[1], w[2])]


def _where(n):
    o, e = lax.axis_index('outer'), lax.axis_index('expert')
    return o // n, o % n, e // 2, e % 2


def _dev(n, z, y, x, c):
    return (0, z * n + y, x * 2 + c)


def _along(n, p, me, a):
    z, y, x, c = me
    return _dev(n, *((a, y, x, c), (z, a, x, c), (z, y, a, c))[p])


def _copy(src, dst, send, recv, dev):
    return pltpu.make_async_remote_copy(src_ref=src, dst_ref=dst, send_sem=send, recv_sem=recv, device_id=dev, device_id_type=MESH)


def _wait(ref, sem):
    pltpu.make_async_copy(ref, ref, sem).wait()


def _dispatch(n, cols, x_ref, meta_ref, xin, meta_out, ag0, ag1, ag2, mb, sb0, sb1, sb2, own, asend, msend, arecv, mrecv, send, recv):
    me = _where(n)
    z, y, x, c = me
    ag, sb = (ag0, ag1, ag2), (sb0, sb1, sb2)
    T = x_ref.shape[0]
    C = sb0.shape[2]
    L = 2 * n * C
    axis = (z, y, x)
    which = (0, 0, 1)
    ring = [1, n - 1] + list(range(2, n - 1)) if n > 2 else [1]
    for p in range(3):
        lo, w = cols[p]
        for k in ring:
            to = _along(n, p, me, (axis[p] + k) % n)
            _copy(meta_ref.at[which[p]], mb.at[p, axis[p]], msend.at[p, k], mrecv.at[p, k], to).start()
            _copy(x_ref.at[:, pl.ds(lo, w)], ag[p].at[axis[p]], asend.at[p, k], arecv.at[p, k], to).start()
        pltpu.make_async_copy(meta_ref.at[which[p]], mb.at[p, axis[p]], msend.at[p, 0]).start()
        pltpu.make_async_copy(x_ref.at[:, pl.ds(lo, w)], ag[p].at[axis[p]], asend.at[p, 0]).start()

    for p in range(3):
        lo, w = cols[p]
        _wait(mb.at[p, 0], msend.at[p, 0])
        _wait(ag[p].at[0], asend.at[p, 0])
        for k in ring:
            _wait(mb.at[p, 0], mrecv.at[p, k])
            _wait(ag[p].at[0], arecv.at[p, k])

        @pl.loop(0, n)
        def _(i):
            b = ((y, z, z)[p] + i) % n
            row = (z * n + b, b * n + y, b * n + x)[p]
            for a in range(n):
                tab = mb[p, a, 0, pl.ds(row, 1), :]
                hot = lax.broadcasted_iota(jnp.int32, (T, L), 0).astype(F32) == tab
                hot = jnp.where(hot, 1.0, 0.0).astype(BF16)
                r = lax.dot_general(hot, ag[p][a], (((0,), (0,)), ((), ())), preferred_element_type=F32)
                sb[p][a, pl.ds(b * 2 * n, 2 * n)] = r.astype(BF16).reshape(2 * n, C, w)
            for jj in range(2 * n):
                d = ((x, x, y)[p] + jj // 2) % n
                cc = (c + jj) % 2
                to = _dev(n, *((z, b, d, cc), (b, y, d, cc), (b, d, x, cc))[p])
                src = sb[p].at[:, b * 2 * n + d * 2 + cc]
                dst = (xin.at[:, y, x, c, :, pl.ds(lo, w)], xin.at[z, :, x, c, :, pl.ds(lo, w)], xin.at[z, y, :, c, :, pl.ds(lo, w)])[p]
                far = _copy(src, dst, send.at[p], recv.at[p], to)
                if jj:
                    far.start()
                else:
                    @pl.when(i == 0)
                    def _():
                        pltpu.make_async_copy(src, dst, own.at[p]).start()

                    @pl.when(i > 0)
                    def _():
                        far.start()

    meta_out[...] = mb[...]
    for p in range(3):
        rest = sb[p].at[:, pl.ds(0, 2 * n * n - 1)]
        for k in ring:
            _wait(mb.at[p, 0], msend.at[p, k])
            _wait(ag[p].at[0], asend.at[p, k])
        _wait(sb[p].at[:, 0], own.at[p])
        _wait(rest, send.at[p])
        _wait(rest, recv.at[p])


def _experts(n, cols, xin, w1_ref, w3_ref, w2_ref, r0, r1, r2, w1, w3, w2, xb, hb, ob, wsem, xsem, own, send, recv):
    me = _where(n)
    z, y, x, c = me
    R = (r0, r1, r2)
    C, D = xin.shape[4:]
    G = 2 * n * C
    ff = w1.shape[1]
    half = n // 2
    steps = n * half
    loads = [pltpu.make_async_copy(s.at[0], d, wsem.at[q]) for q, (s, d) in enumerate(((w1_ref, w1), (w3_ref, w3), (w2_ref, w2)))]

    def place(s):
        jp = s % half
        return (z + s // half) % n, (y + 2 * jp) % n, (y + 2 * jp + 1) % n

    def load(s):
        zt, y0, y1 = place(s)
        return [pltpu.make_async_copy(xin.at[zt, yv], xb.at[s % 2, q], xsem.at[s % 2, q]) for q, yv in enumerate((y0, y1))]

    for q in load(0):
        q.start()
    for q in loads:
        q.start()
    mine = (y * 2 * n + x * 2 + c, z * 2 * n + x * 2 + c, z * 2 * n + y * 2 + c)

    def out(p, src, dst, to, local):
        far = _copy(src, dst, send.at[p], recv.at[p], to)
        if local is None:
            far.start()
            return

        @pl.when(local)
        def _():
            pltpu.make_async_copy(src, dst, own.at[p]).start()

        @pl.when(jnp.logical_not(local))
        def _():
            far.start()

    fs, ds = min(256, ff), min(512, D)
    cs = [pl.ds(lo, w) for lo, w in cols]

    @pl.loop(0, steps)
    def _(s):
        zt, y0, y1 = place(s)
        i, jp = s // half, s % half

        @pl.when(s + 1 < steps)
        def _():
            for q in load(s + 1):
                q.start()

        for q in load(s):
            q.wait()

        @pl.when(s == 0)
        def _():
            for q in loads:
                q.wait()

        @pl.loop(0, ff // fs)
        def _(f):
            fc = pl.ds(pl.multiple_of(f * fs, fs), fs)
            xt = xb[s % 2].reshape(2 * G, D)
            a = jnp.dot(xt, w1[:, fc], preferred_element_type=F32)
            b = jnp.dot(xt, w3[:, fc], preferred_element_type=F32)
            hb[:, fc] = (jax.nn.silu(a) * b).astype(BF16)

        @pl.loop(0, D // ds)
        def _(f):
            fc = pl.ds(pl.multiple_of(f * ds, ds), ds)
            o = jnp.dot(hb[...], w2[:, fc], preferred_element_type=F32).astype(BF16)
            ob[zt, y0, :, :, :, fc] = o[:G].reshape(n, 2, C, ds)
            ob[zt, y1, :, :, :, fc] = o[G:].reshape(n, 2, C, ds)

        for q, yv in enumerate((y0, y1)):
            for cc in range(2):
                c2 = (c + cc) % 2
                out(2, ob.at[zt, yv, :, c2, :, cs[2]], R[2].at[:, mine[2]], _dev(n, zt, yv, x, c2), (s == 0) if q + cc == 0 else None)
            for d in range(n):
                for cc in range(2):
                    x2, c2 = (x + d) % n, (c + cc) % 2
                    out(0, ob.at[zt, yv, x2, c2, :, cs[0]], R[0].at[zt, mine[0]], _dev(n, z, yv, x2, c2), (jp == 0) if q + d + cc == 0 else None)

        @pl.when(jp == half - 1)
        def _():
            for d in range(n):
                for cc in range(2):
                    x2, c2 = (x + d) % n, (c + cc) % 2
                    out(1, ob.at[zt, :, x2, c2, :, cs[1]], R[1].at[:, mine[1]], _dev(n, zt, y, x2, c2), (i == 0) if d + cc == 0 else None)

    for p in range(3):
        rest = R[p].at[:, pl.ds(0, 2 * n * n - 1)]
        _wait(R[p].at[:, 0], own.at[p])
        _wait(rest, send.at[p])
        _wait(rest, recv.at[p])


def _combine(n, cols, r0, r1, r2, meta, y_ref, b0, b1, b2, p0, p1, p2, q0, q1, q2, rsem, send, recv):
    me = _where(n)
    z, y, x, c = me
    R, B, S, Q = (r0, r1, r2), (b0, b1, b2), (p0, p1, p2), (q0, q1, q2)
    axis = (z, y, x)
    T = y_ref.shape[0]
    C = b0.shape[2]
    L = 2 * n * C
    for p in range(3):
        pltpu.make_async_copy(R[p], B[p], rsem.at[p]).start()
    for p in range(3):
        lo, w = cols[p]
        _wait(B[p], rsem.at[p])

        @pl.loop(0, n)
        def _(k):
            k = (k + 1) % n
            a = (axis[p] + k) % n

            for b in range(n):
                row = (z * n + b, b * n + y, b * n + x)[p]
                tab = meta[p, a, 0, pl.ds(row, 1), :]
                g = meta[p, a, 1, pl.ds(row, 1), :]
                hot = lax.broadcasted_iota(jnp.int32, (T, L), 0).astype(F32) == tab
                m = jnp.where(hot, g, 0.0)
                hi = m.astype(BF16)
                m = m - hi.astype(F32)
                mid = m.astype(BF16)
                low = (m - mid.astype(F32)).astype(BF16)
                v = B[p][a, pl.ds(b * 2 * n, 2 * n)].reshape(L, w)
                t = jnp.dot(hi, v, preferred_element_type=F32)
                t += jnp.dot(mid, v, preferred_element_type=F32)
                t += jnp.dot(low, v, preferred_element_type=F32)
                if b == 0:
                    S[p][k] = t
                else:
                    S[p][k] += t

            @pl.when(k > 0)
            def _():
                _copy(S[p].at[k], Q[p].at[k - 1], send.at[p, k], recv.at[p, k], _along(n, p, me, a)).start()

    for p in range(3):
        lo, w = cols[p]
        t = S[p][0]
        for k in range(1, n):
            _wait(Q[p].at[k - 1], recv.at[p, k])
            t += Q[p][k - 1]
        y_ref[:, pl.ds(lo, w)] = t.astype(BF16)
    for p in range(3):
        for k in range(1, n):
            _wait(Q[p].at[k - 1], send.at[p, k])


def _plan(x, wr, idx, n, cap):
    T = x.shape[0]
    E = wr.shape[1]
    logits = jnp.dot(x, wr, preferred_element_type=F32)
    oh = idx[:, :, None] == jnp.arange(E, dtype=idx.dtype)
    g = jax.nn.softmax(jnp.sum(jnp.where(oh, logits[:, None, :], 0.0), axis=-1), axis=-1)
    m = jnp.sum(oh, axis=1, dtype=jnp.int32).astype(F32)
    ge = jnp.sum(jnp.where(oh, g[:, :, None], 0.0), axis=1)
    pos = jnp.arange(T, dtype=jnp.int32)
    tri = (pos[None, :] < pos[:, None]).astype(BF16)
    cnt = jnp.dot(tri, m.astype(BF16), preferred_element_type=F32)
    cnt = jnp.where(m > 0, cnt, -1.0)
    hit = cnt[:, :, None] == jnp.arange(cap, dtype=F32)
    tab = jnp.sum(jnp.where(hit, pos.astype(F32)[:, None, None] + 1.0, 0.0), axis=0) - 1.0
    gw = jnp.sum(jnp.where(hit, ge[:, :, None], 0.0), axis=0)

    def both(v):
        v = v.reshape(n, n, n, 2 * cap)
        return v.reshape(n * n, 2 * n * cap), v.transpose(0, 2, 1, 3).reshape(n * n, 2 * n * cap)

    (t0, t2), (g0, g2) = both(tab), both(gw)
    return jnp.stack([jnp.stack([t0, g0]), jnp.stack([t2, g2])])


def solution(mesh):
    O, X = mesh.shape['outer'], mesh.shape['expert']
    n = X // 2
    tok = P(('data', 'outer', 'expert'), None)
    wsp = P(('outer', 'expert'), None, None)
    any_ = pl.BlockSpec(memory_space=pl.ANY)
    vmem = pl.BlockSpec(memory_space=pltpu.VMEM)
    dma = pltpu.SemaphoreType.DMA
    params = pltpu.CompilerParams(has_side_effects=True, vmem_limit_bytes=60 * 1024 * 1024)

    def local(x, wr, idx, w1, w3, w2):
        T, D = x.shape
        E = wr.shape[1]
        C = 2 * T * idx.shape[1] // E
        ff = w1.shape[2]
        cols = _cols(D)
        widths = [w for _, w in cols]
        L = 2 * n * C
        blocks = [(n, 2 * n * n, C, w) for w in widths]
        meta = _plan(x, wr, idx, n, C)
        xin, metas = pl.pallas_call(
            functools.partial(_dispatch, n, cols),
            name='dispatch',
            out_shape=[jax.ShapeDtypeStruct((n, n, n, 2, C, D), BF16), jax.ShapeDtypeStruct((3, n, 2, n * n, L), F32)],
            in_specs=[any_, any_],
            out_specs=[any_, vmem],
            scratch_shapes=[pltpu.VMEM((n, T, w), BF16) for w in widths] + [pltpu.VMEM((3, n, 2, n * n, L), F32)]
            + [pltpu.VMEM(b, BF16) for b in blocks]
            + [dma((3,)), dma((3, n)), dma((3, n)), dma((3, n)), dma((3, n)), dma((3,)), dma((3,))],
            compiler_params=params,
        )(x, meta)
        r = pl.pallas_call(
            functools.partial(_experts, n, cols),
            name='experts',
            out_shape=[jax.ShapeDtypeStruct(b, BF16) for b in blocks],
            in_specs=[any_] * 4,
            out_specs=[any_] * 3,
            scratch_shapes=[
                pltpu.VMEM((D, ff), BF16), pltpu.VMEM((D, ff), BF16), pltpu.VMEM((ff, D), BF16),
                pltpu.VMEM((2, 2, n, 2, C, D), BF16), pltpu.VMEM((2 * L, ff), BF16), pltpu.VMEM((n, n, n, 2, C, D), BF16),
                dma((3,)), dma((2, 2)), dma((3,)), dma((3,)), dma((3,)),
            ],
            compiler_params=params,
        )(xin, w1, w3, w2)
        return pl.pallas_call(
            functools.partial(_combine, n, cols),
            name='combine',
            out_shape=jax.ShapeDtypeStruct((T, D), BF16),
            in_specs=[any_] * 3 + [vmem],
            out_specs=vmem,
            scratch_shapes=[pltpu.VMEM(b, BF16) for b in blocks]
            + [pltpu.VMEM((n, T, w), F32) for w in widths] + [pltpu.VMEM((n - 1, T, w), F32) for w in widths]
            + [dma((3,)), dma((3, n)), dma((3, n))],
            compiler_params=params,
        )(*r, metas)

    return jax.shard_map(local, mesh=mesh, in_specs=(tok, P(None, None), tok, wsp, wsp, wsp), out_specs=tok, check_vma=False)
```

time: 609 us -> 520 us (0.85)
  the two profiles are of different devices: /device:TPU:2 before, /device:TPU:0 now
where the time goes in v2:
time: 520 us
  Pallas kernels  510 us (98%)
    pallas_call x1, Pallas kernels, local(): pl.pallas_call(functools.partial(_experts, n, cols), name='experts', out_...  233 us
    pallas_call x1, Pallas kernels, local(): pl.pallas_call(functools.partial(_dispatch, n, cols), name='dispatch', ou...  220 us
    pallas_call x1, Pallas kernels, local(): pl.pallas_call(functools.partial(_combine, n, cols), name='combine', out_...  56.6 us

profile of v2, /device:TPU:0, one launch (start us, length us, event | category | flops | bytes accessed | tf_op | source)
XLA Modules:
  0.0 519.8 jit_solution(9413986849389069734)
XLA Ops:
  0.0 0.0 copy-start
  0.0 0.9 copy.22
  0.9 0.4 convert_reduce_fusion
  1.3 0.2 convolution_select_fusion
  1.5 0.0 copy-done
  1.5 1.7 fusion.2
  3.1 0.9 select_reduce_fusion.3
  4.0 0.1 reduce_max.9
  4.1 0.1 copy.25
  4.3 0.1 copy.26
  4.4 1.3 select_reduce_fusion.2
  5.7 0.7 select_reduce_fusion.1
  6.4 0.1 copy.23
  6.5 0.1 sub.21
  6.6 0.1 sub.24
  6.7 0.1 stack_reshape.6
  6.8 0.1 copy.27
  6.9 0.1 stack_reshape_reshape.4
  6.9 0.1 reshape.64
  7.0 0.1 stack_reshape.7
  7.1 0.6 pad_maximum_fusion.meta_ref
  7.8 220.2 %dispatch.1 = (bf16[4,4,4,2,32,2048]{5,4,3,2,1,0:T(8,128)(2,1)}, f32[3,4,2,16,256]{4,3,2,1,0:T(8,128)}) custom-call(bf16[256,2048]{1,0:T(8,128)(2,1)} %x_ref.1, f32[2,2,16,256]{3,2,1,0:T(8,128)} %pad_maximum_fusion.meta_ref), custom_call_target="tpu_custom_call" | custom-call | tf_op jit(solution)/shard_map/dispatch/pallas_call | solution.py:305
  228.0 232.8 %experts.1 = (bf16[4,32,32,640]{3,2,1,0:T(8,128)(2,1)}, bf16[4,32,32,640]{3,2,1,0:T(8,128)(2,1)}, bf16[4,32,32,768]{3,2,1,0:T(8,128)(2,1)}) custom-call(bf16[4,4,4,2,32,2048]{5,4,3,2,1,0:T(8,128)(2,1)} %get-tuple-element.10.xin, bf16[1,2048,768]{2,1,0:T(8,128)(2,1)} %w1_ref.1, bf16[1,2048,768]{2,1,0:T(8,128)(2,1)} %w3_ref.1, bf16[1,768,2048]{2,1,0:T(8,128)(2,1)} %w2_ref.1), custom_call_target="tpu_custom_call" | custom-call | tf_op jit(solution)/shard_map/experts/pallas_call | solution.py:316
  460.9 56.6 %combine.1 = bf16[256,2048]{1,0:T(8,128)(2,1)} custom-call(bf16[4,32,32,640]{3,2,1,0:T(8,128)(2,1)} %get-tuple-element.11.r0, bf16[4,32,32,640]{3,2,1,0:T(8,128)(2,1)} %get-tuple-element.12.r1, bf16[4,32,32,768]{3,2,1,0:T(8,128)(2,1)} %get-tuple-element.13.r2, f32[3,4,2,16,256]{4,3,2,1,0:T(8,128)} %get-tuple-element.14.meta), custom_call_target="tpu_custom_call" | custom-call | tf_op jit(solution)/shard_map/combine/pallas_call | solution.py:329
  517.5 2.3 copy.34
  (7 shorter events, 0.1 us)
Async XLA Ops:
  0.0 1.5 copy-start

commit v3 on v2

v3 whole, which is shorter than its diff:
```python
import functools

import jax
import jax.numpy as jnp
from jax import lax
from jax.experimental import pallas as pl
from jax.experimental.pallas import tpu as pltpu
from jax.sharding import PartitionSpec as P

MESH = pl.DeviceIdType.MESH
F32 = jnp.float32
BF16 = jnp.bfloat16
N = 4


def _cols(d):
    t = d // 128
    w = [(t // 3) * 128, (t // 3) * 128, (t - 2 * (t // 3)) * 128]
    return [(0, w[0]), (w[0], w[1]), (w[0] + w[1], w[2])]


def _where():
    o, e = lax.axis_index('outer'), lax.axis_index('expert')
    return o // N, o % N, e // 2, e % 2


def _dev(z, y, x, c):
    return (0, z * N + y, x * 2 + c)


def _along(p, me, a):
    z, y, x, c = me
    return _dev(*((a, y, x, c), (z, a, x, c), (z, y, a, c))[p])


def _plane(p, me, b, d, c):
    z, y, x, _ = me
    return _dev(*((z, b, d, c), (b, y, d, c), (b, d, x, c))[p])


def _copy(src, dst, send, recv, dev):
    return pltpu.make_async_remote_copy(src_ref=src, dst_ref=dst, send_sem=send, recv_sem=recv, device_id=dev, device_id_type=MESH)


def _wait(ref, sem):
    pltpu.make_async_copy(ref, ref, sem).wait()


def _far(o):
    return int(o == 2)


RELAYED = [(b, d, cc) for b in (2, 1, 3, 0) for d in (2, 1, 3, 0) for cc in range(2) if 2 in (b, d)]
NEAR = N * N * 2 - len(RELAYED) - 1


def _forward(p, me, base, rel, rsem, final, fsend, recv):
    c = me[3]
    for b, d, cc in RELAYED:
        s = 1 - 2 * cc
        bs, ds = (base[0] + N - s * _far(b)) % N, (base[1] + N - s * _far(d)) % N
        key = (b * N + d) * 2 + cc
        _wait(rel.at[:, key], rsem.at[p, key])
        to = _plane(p, me, (bs + b) % N, (ds + d) % N, (c + cc) % 2)
        _copy(rel.at[:, key], final(p, bs, ds), fsend.at[p], recv.at[p], to).start()


def _dispatch(cols, x_ref, meta_ref, xin, meta_out, ag0, ag1, ag2, mb, sb0, sb1, sb2, rl0, rl1, rl2,
              own, lown, asend, msend, arecv, mrecv, lsend, send, fsend, rrecv, recv):
    me = _where()
    z, y, x, c = me
    ag, sb, rl = (ag0, ag1, ag2), (sb0, sb1, sb2), (rl0, rl1, rl2)
    T = x_ref.shape[0]
    C = sb0.shape[2]
    L = 2 * N * C
    h = T // 2
    axis = (z, y, x)
    base = ((y, x), (z, x), (z, y))
    which = (0, 0, 1)
    for p in range(3):
        lo, w = cols[p]
        at = axis[p]
        blk = x_ref.at[:, pl.ds(lo, w)]
        for k in range(2):
            _copy(blk, ag[p].at[at], asend.at[p, k], arecv.at[p, k], _along(p, me, (at + (1, 3)[k]) % N)).start()
        pltpu.make_async_copy(blk, ag[p].at[at], lown.at[p, 0]).start()
    for p in range(3):
        at = axis[p]
        for k in (1, 3, 2):
            _copy(meta_ref.at[which[p]], mb.at[p, at], msend.at[p, k], mrecv.at[p, k], _along(p, me, (at + k) % N)).start()
        pltpu.make_async_copy(meta_ref.at[which[p]], mb.at[p, at], lown.at[p, 1]).start()
    halves = (pl.ds(0, h), pl.ds(h, h))
    for p in range(3):
        at = axis[p]
        for k in range(2):
            _wait(ag[p].at[0], arecv.at[p, k])
            part = ag[p].at[(at + (3, 1)[k]) % N, halves[k]]
            _copy(part, part, asend.at[p, 2 + k], arecv.at[p, 2 + k], _along(p, me, (at + (1, 3)[k]) % N)).start()

    def final(p, b, d):
        cs = pl.ds(*cols[p])
        return (xin.at[:, b, d, c, :, cs], xin.at[b, :, d, c, :, cs], xin.at[b, d, :, c, :, cs])[p]

    for p in range(3):
        w = cols[p][1]
        bm, dm = base[p]
        _wait(mb.at[p, 0], lown.at[p, 1])
        _wait(ag[p].at[0], lown.at[p, 0])
        for k in (1, 3, 2):
            _wait(mb.at[p, 0], mrecv.at[p, k])
        for k in range(2):
            _wait(ag[p].at[0, halves[k]], arecv.at[p, 2 + k])

        @pl.loop(0, N)
        def _(i):
            bo = (2 + 3 * i) % N
            b = (bm + bo) % N
            row = (z * N + b, b * N + y, b * N + x)[p]

            for a in range(N):
                tab = mb[p, a, 0, pl.ds(row, 1), :]
                hot = lax.broadcasted_iota(jnp.int32, (T, L), 0).astype(F32) == tab
                hot = jnp.where(hot, 1.0, 0.0).astype(BF16)
                r = lax.dot_general(hot, ag[p][a], (((0,), (0,)), ((), ())), preferred_element_type=F32)
                sb[p][a, pl.ds(b * 2 * N, 2 * N)] = r.astype(BF16).reshape(2 * N, C, w)
            for do in (2, 1, 3, 0):
                for cc in range(2):
                    s = 1 - 2 * cc
                    d = (dm + do) % N
                    fb = (N - 1 - i) // (N - 1)
                    to = _plane(p, me, (bm + N + s * fb) % N, (dm + N + s * _far(do)) % N, c)
                    leg = _copy(sb[p].at[:, b * 2 * N + d * 2 + (c + cc) % 2], rl[p].at[:, (bo * N + do) * 2 + cc],
                                lsend.at[p], rrecv.at[p, (bo * N + do) * 2 + cc], to)
                    if _far(do):
                        leg.start()
                    else:
                        @pl.when(i == 0)
                        def _():
                            leg.start()

    for bo in (1, 3, 0):
        for do in (1, 3, 0):
            for cc in range(2):
                for p in range(3):
                    bm, dm = base[p]
                    b, d, c2 = (bm + bo) % N, (dm + do) % N, (c + cc) % 2
                    src = sb[p].at[:, b * 2 * N + d * 2 + c2]
                    if bo + do + cc == 0:
                        pltpu.make_async_copy(src, final(p, bm, dm), own.at[p]).start()
                    else:
                        _copy(src, final(p, bm, dm), send.at[p], recv.at[p], _plane(p, me, b, d, c2)).start()
    meta_out[...] = mb[...]
    for p in range(3):
        _forward(p, me, base[p], rl[p], rrecv, final, fsend, recv)
    for p in range(3):
        for k in (1, 2, 3):
            _wait(mb.at[p, 0], msend.at[p, k])
        for k in range(2):
            _wait(ag[p].at[0], asend.at[p, k])
            _wait(ag[p].at[0, halves[k]], asend.at[p, 2 + k])
        _wait(sb[p].at[:, 0], own.at[p])
        _wait(sb[p].at[:, pl.ds(0, NEAR)], send.at[p])
        _wait(sb[p].at[:, pl.ds(0, len(RELAYED))], lsend.at[p])
        _wait(sb[p].at[:, pl.ds(0, len(RELAYED))], fsend.at[p])
        _wait(sb[p].at[:, pl.ds(0, NEAR + len(RELAYED))], recv.at[p])


def _experts(cols, xin, w1_ref, w3_ref, w2_ref, r0, r1, r2, w1, w3, w2, xb, hb, ob, rl0, rl1, rl2,
             wsem, xsem, own, lsend, send, fsend, rrecv, recv):
    me = _where()
    z, y, x, c = me
    R, rl = (r0, r1, r2), (rl0, rl1, rl2)
    C, D = xin.shape[4:]
    G = 2 * N * C
    ff = w1.shape[1]
    half = N // 2
    steps = N * half
    base = ((y, x), (z, x), (z, y))
    loads = [pltpu.make_async_copy(s.at[0], d, wsem.at[q]) for q, (s, d) in enumerate(((w1_ref, w1), (w3_ref, w3), (w2_ref, w2)))]

    def place(s):
        zo = (2 + 3 * (s // half)) % N
        yo = [(2 + 2 * (s % half) + 3 * q) % N for q in range(2)]
        return (z + zo) % N, zo, [(y + o) % N for o in yo], yo

    def load(s):
        zt, _, ys, _ = place(s)
        return [pltpu.make_async_copy(xin.at[zt, yv], xb.at[s % 2, q], xsem.at[s % 2, q]) for q, yv in enumerate(ys)]

    for q in load(0):
        q.start()
    for q in loads:
        q.start()
    cs = [pl.ds(lo, w) for lo, w in cols]

    def final(p, b, d):
        return R[p].at[:, (b * N + d) * 2 + c]

    def put(p, src, bo, do, fb, fd, cc, lead, relay, self_):
        bm, dm = base[p]
        s = 1 - 2 * cc
        key = (bo * N + do) * 2 + cc
        leg = _copy(src, rl[p].at[lead, key], lsend.at[p], rrecv.at[p, key],
                    _plane(p, me, (bm + N + s * fb) % N, (dm + N + s * fd) % N, c))
        dst = R[p].at[lead, (bm * N + dm) * 2 + c]
        far = _copy(src, dst, send.at[p], recv.at[p], _plane(p, me, (bm + bo) % N, (dm + do) % N, (c + cc) % 2))
        near = pltpu.make_async_copy(src, dst, own.at[p])
        if relay is True:
            leg.start()
            return

        def direct():
            if self_ is None:
                far.start()
                return

            @pl.when(self_)
            def _():
                near.start()

            @pl.when(jnp.logical_not(self_))
            def _():
                far.start()

        if relay is None:
            direct()
            return

        @pl.when(relay)
        def _():
            leg.start()

        @pl.when(jnp.logical_not(relay))
        def _():
            direct()

    fs, ds = min(256, ff), min(512, D)
    every = slice(None)

    @pl.loop(0, steps)
    def _(s):
        zt, zo, ys, yo = place(s)
        i, jp = s // half, s % half
        fz = (N - 1 - i) // (N - 1)

        @pl.when(s + 1 < steps)
        def _():
            for q in load(s + 1):
                q.start()

        for q in load(s):
            q.wait()

        @pl.when(s == 0)
        def _():
            for q in loads:
                q.wait()

        @pl.loop(0, ff // fs)
        def _(f):
            fc = pl.ds(pl.multiple_of(f * fs, fs), fs)
            xt = xb[s % 2].reshape(2 * G, D)
            a = jnp.dot(xt, w1[:, fc], preferred_element_type=F32)
            b = jnp.dot(xt, w3[:, fc], preferred_element_type=F32)
            hb[:, fc] = (jax.nn.silu(a) * b).astype(BF16)

        @pl.loop(0, D // ds)
        def _(f):
            fc = pl.ds(pl.multiple_of(f * ds, ds), ds)
            o = jnp.dot(hb[...], w2[:, fc], preferred_element_type=F32).astype(BF16)
            ob[zt, ys[0], :, :, :, fc] = o[:G].reshape(N, 2, C, ds)
            ob[zt, ys[1], :, :, :, fc] = o[G:].reshape(N, 2, C, ds)

        for q in range(2):
            fy = 1 - jp if q == 0 else 0
            for cc in range(2):
                put(2, ob.at[zt, ys[q], :, (c + cc) % 2, :, cs[2]], zo, yo[q], fz, fy, cc, every,
                    (i == 0) if q else (fz + fy > 0), (s == 2 * half + 1) if q + cc == 0 else None)
            for do in (2, 1, 3, 0):
                for cc in range(2):
                    put(0, ob.at[zt, ys[q], (x + do) % N, (c + cc) % 2, :, cs[0]], yo[q], do, fy, _far(do), cc, zt,
                        True if _far(do) else (None if q else (jp == 0)), (jp == 1) if q + do + cc == 0 else None)

        @pl.when(jp == half - 1)
        def _():
            for do in (2, 1, 3, 0):
                for cc in range(2):
                    put(1, ob.at[zt, :, (x + do) % N, (c + cc) % 2, :, cs[1]], zo, do, fz, _far(do), cc, every,
                        True if _far(do) else (i == 0), (i == 2) if do + cc == 0 else None)

    for p in (2, 1, 0):
        _forward(p, me, base[p], rl[p], rrecv, final, fsend, recv)
    for p in range(3):
        _wait(R[p].at[:, 0], own.at[p])
        _wait(R[p].at[:, pl.ds(0, NEAR)], send.at[p])
        _wait(R[p].at[:, pl.ds(0, len(RELAYED))], lsend.at[p])
        _wait(R[p].at[:, pl.ds(0, len(RELAYED))], fsend.at[p])
        _wait(R[p].at[:, pl.ds(0, NEAR + len(RELAYED))], recv.at[p])


def _combine(cols, r0, r1, r2, meta, y_ref, b0, b1, b2, p0, p1, p2, q0, q1, q2, h0, h1, h2, mw, rsem, send, recv):
    me = _where()
    z, y, x, c = me
    R, B, S, Q, H = (r0, r1, r2), (b0, b1, b2), (p0, p1, p2), (q0, q1, q2), (h0, h1, h2)
    axis = (z, y, x)
    T = y_ref.shape[0]
    C = b0.shape[2]
    L = 2 * N * C
    h = T // 2
    halves = (pl.ds(0, h), pl.ds(h, h))
    for p in range(3):
        for k in (2, 1, 3, 0):
            a = (axis[p] + k) % N
            pltpu.make_async_copy(R[p].at[a], B[p].at[a], rsem.at[p, k]).start()

    def partial(p, k):
        a = (axis[p] + k) % N
        _wait(B[p].at[0], rsem.at[p, k])

        @pl.loop(0, N)
        def _(b):
            row = (z * N + b, b * N + y, b * N + x)[p]
            tab = meta[p, a, 0, pl.ds(row, 1), :]
            g = meta[p, a, 1, pl.ds(row, 1), :]
            hot = lax.broadcasted_iota(jnp.int32, (T, L), 0).astype(F32) == tab
            m = jnp.where(hot, g, 0.0)
            here = pl.ds(pl.multiple_of(b * L, L), L)
            for q in range(3):
                part = m.astype(BF16)
                mw[q * T:(q + 1) * T, here] = part
                m = m - part.astype(F32)

        v = B[p][a].reshape(N * L, cols[p][1])
        t = jnp.dot(mw[...], v, preferred_element_type=F32)
        S[p][k] = t[:T] + t[T:2 * T] + t[2 * T:]

    def side(p, k):
        return _along(p, me, (axis[p] + (1, 3)[k]) % N)

    for p in range(3):
        partial(p, 2)
        for k in range(2):
            _copy(S[p].at[2, halves[k]], H[p].at[k], send.at[p, k], recv.at[p, k], side(p, k)).start()
    for p in range(3):
        for k in range(2):
            partial(p, (1, 3)[k])
            _wait(H[p].at[k], recv.at[p, k])
            S[p][(1, 3)[k], halves[k]] += H[p][k]
            _copy(S[p].at[(1, 3)[k]], Q[p].at[k], send.at[p, 2 + k], recv.at[p, 2 + k], side(p, k)).start()
    for p in range(3):
        partial(p, 0)
    for p in range(3):
        t = S[p][0]
        for k in range(2):
            _wait(Q[p].at[k], recv.at[p, 2 + k])
            t += Q[p][k]
        y_ref[:, pl.ds(*cols[p])] = t.astype(BF16)
    for p in range(3):
        for k in range(2):
            _wait(H[p].at[k], send.at[p, k])
            _wait(Q[p].at[k], send.at[p, 2 + k])


def _plan(x, wr, idx, cap):
    T = x.shape[0]
    E = wr.shape[1]
    logits = jnp.dot(x, wr, preferred_element_type=F32)
    oh = idx[:, :, None] == jnp.arange(E, dtype=idx.dtype)
    g = jax.nn.softmax(jnp.sum(jnp.where(oh, logits[:, None, :], 0.0), axis=-1), axis=-1)
    m = jnp.sum(oh, axis=1, dtype=jnp.int32).astype(F32)
    ge = jnp.sum(jnp.where(oh, g[:, :, None], 0.0), axis=1)
    pos = jnp.arange(T, dtype=jnp.int32)
    tri = (pos[None, :] < pos[:, None]).astype(BF16)
    cnt = jnp.dot(tri, m.astype(BF16), preferred_element_type=F32)
    cnt = jnp.where(m > 0, cnt, -1.0)
    hit = cnt[:, :, None] == jnp.arange(cap, dtype=F32)
    tab = jnp.sum(jnp.where(hit, pos.astype(F32)[:, None, None] + 1.0, 0.0), axis=0) - 1.0
    gw = jnp.sum(jnp.where(hit, ge[:, :, None], 0.0), axis=0)

    def both(v):
        v = v.reshape(N, N, N, 2 * cap)
        return v.reshape(N * N, 2 * N * cap), v.transpose(0, 2, 1, 3).reshape(N * N, 2 * N * cap)

    (t0, t2), (g0, g2) = both(tab), both(gw)
    return jnp.stack([jnp.stack([t0, g0]), jnp.stack([t2, g2])])


def solution(mesh):
    assert (mesh.shape['outer'], mesh.shape['expert']) == (N * N, 2 * N)
    tok = P(('data', 'outer', 'expert'), None)
    wsp = P(('outer', 'expert'), None, None)
    any_ = pl.BlockSpec(memory_space=pl.ANY)
    vmem = pl.BlockSpec(memory_space=pltpu.VMEM)
    dma = pltpu.SemaphoreType.DMA
    params = pltpu.CompilerParams(has_side_effects=True, vmem_limit_bytes=60 * 1024 * 1024)

    def local(x, wr, idx, w1, w3, w2):
        T, D = x.shape
        E = wr.shape[1]
        C = 2 * T * idx.shape[1] // E
        ff = w1.shape[2]
        cols = _cols(D)
        widths = [w for _, w in cols]
        L = 2 * N * C
        K = 2 * N * N
        blocks = [(N, K, C, w) for w in widths]
        held = [pltpu.VMEM(b, BF16) for b in blocks]
        meta = _plan(x, wr, idx, C)
        xin, metas = pl.pallas_call(
            functools.partial(_dispatch, cols),
            name='dispatch',
            out_shape=[jax.ShapeDtypeStruct((N, N, N, 2, C, D), BF16), jax.ShapeDtypeStruct((3, N, 2, N * N, L), F32)],
            in_specs=[any_, any_],
            out_specs=[any_, vmem],
            scratch_shapes=[pltpu.VMEM((N, T, w), BF16) for w in widths] + [pltpu.VMEM((3, N, 2, N * N, L), F32)] + held + held
            + [dma((3,)), dma((3, 2)), dma((3, 4)), dma((3, 4)), dma((3, 4)), dma((3, 4)), dma((3,)), dma((3,)), dma((3,)), dma((3, K)), dma((3,))],
            compiler_params=params,
        )(x, meta)
        r = pl.pallas_call(
            functools.partial(_experts, cols),
            name='experts',
            out_shape=[jax.ShapeDtypeStruct(b, BF16) for b in blocks],
            in_specs=[any_] * 4,
            out_specs=[any_] * 3,
            scratch_shapes=[
                pltpu.VMEM((D, ff), BF16), pltpu.VMEM((D, ff), BF16), pltpu.VMEM((ff, D), BF16),
                pltpu.VMEM((2, 2, N, 2, C, D), BF16), pltpu.VMEM((2 * L, ff), BF16), pltpu.VMEM((N, N, N, 2, C, D), BF16), *held,
                dma((3,)), dma((2, 2)), dma((3,)), dma((3,)), dma((3,)), dma((3,)), dma((3, K)), dma((3,)),
            ],
            compiler_params=params,
        )(xin, w1, w3, w2)
        return pl.pallas_call(
            functools.partial(_combine, cols),
            name='combine',
            out_shape=jax.ShapeDtypeStruct((T, D), BF16),
            in_specs=[any_] * 3 + [vmem],
            out_specs=vmem,
            scratch_shapes=held + [pltpu.VMEM((N, T, w), F32) for w in widths] + [pltpu.VMEM((2, T, w), F32) for w in widths]
            + [pltpu.VMEM((2, T // 2, w), F32) for w in widths] + [pltpu.VMEM((3 * T, N * L), BF16), dma((3, N)), dma((3, 4)), dma((3, 4))],
            compiler_params=params,
        )(*r, metas)

    return jax.shard_map(local, mesh=mesh, in_specs=(tok, P(None, None), tok, wsp, wsp, wsp), out_specs=tok, check_vma=False)
```

time: 520 us -> 451 us (0.87)
  Pallas kernels: 510 us -> 441 us
    pallas_call x3, Pallas kernels: 510 us -> 441 us  [the longest x1 199 us: local(): pl.pallas_call(functools.partial(_experts, cols), name='experts', out_sha...]
where the time goes in v3:
time: 451 us
  Pallas kernels  441 us (98%)
    pallas_call x1, Pallas kernels, local(): pl.pallas_call(functools.partial(_experts, cols), name='experts', out_sha...  199 us
    pallas_call x1, Pallas kernels, local(): pl.pallas_call(functools.partial(_dispatch, cols), name='dispatch', out_s...  186 us
    pallas_call x1, Pallas kernels, local(): pl.pallas_call(functools.partial(_combine, cols), name='combine', out_sha...  56.4 us

profile of v3, /device:TPU:0, one launch (start us, length us, event | category | flops | bytes accessed | tf_op | source)
XLA Modules:
  0.0 451.1 jit_solution(15002397516067156747)
XLA Ops:
  0.0 0.0 copy-start
  0.0 0.9 copy.22
  0.9 0.4 convert_reduce_fusion
  1.3 0.2 convolution_select_fusion
  1.5 0.0 copy-done
  1.5 1.7 fusion.2
  3.1 0.9 select_reduce_fusion.3
  4.0 0.1 reduce_max.9
  4.1 0.1 copy.25
  4.3 0.1 copy.26
  4.4 1.3 select_reduce_fusion.2
  5.7 0.7 select_reduce_fusion.1
  6.4 0.1 copy.23
  6.5 0.1 sub.21
  6.6 0.1 sub.24
  6.7 0.1 stack_reshape.6
  6.8 0.1 copy.27
  6.9 0.1 stack_reshape_reshape.4
  6.9 0.1 reshape.64
  7.0 0.1 stack_reshape.7
  7.1 0.6 pad_maximum_fusion.meta_ref
  7.8 186.0 %dispatch.1 = (bf16[4,4,4,2,32,2048]{5,4,3,2,1,0:T(8,128)(2,1)}, f32[3,4,2,16,256]{4,3,2,1,0:T(8,128)}) custom-call(bf16[256,2048]{1,0:T(8,128)(2,1)} %x_ref.1, f32[2,2,16,256]{3,2,1,0:T(8,128)} %pad_maximum_fusion.meta_ref), custom_call_target="tpu_custom_call" | custom-call | tf_op jit(solution)/shard_map/dispatch/pallas_call | solution.py:409
  193.7 198.7 %experts.1 = (bf16[4,32,32,640]{3,2,1,0:T(8,128)(2,1)}, bf16[4,32,32,640]{3,2,1,0:T(8,128)(2,1)}, bf16[4,32,32,768]{3,2,1,0:T(8,128)(2,1)}) custom-call(bf16[4,4,4,2,32,2048]{5,4,3,2,1,0:T(8,128)(2,1)} %get-tuple-element.10.xin, bf16[1,2048,768]{2,1,0:T(8,128)(2,1)} %w1_ref.1, bf16[1,2048,768]{2,1,0:T(8,128)(2,1)} %w3_ref.1, bf16[1,768,2048]{2,1,0:T(8,128)(2,1)} %w2_ref.1), custom_call_target="tpu_custom_call" | custom-call | tf_op jit(solution)/shard_map/experts/pallas_call | solution.py:419
  392.4 56.4 %combine.1 = bf16[256,2048]{1,0:T(8,128)(2,1)} custom-call(bf16[4,32,32,640]{3,2,1,0:T(8,128)(2,1)} %get-tuple-element.11.r0, bf16[4,32,32,640]{3,2,1,0:T(8,128)(2,1)} %get-tuple-element.12.r1, bf16[4,32,32,768]{3,2,1,0:T(8,128)(2,1)} %get-tuple-element.13.r2, f32[3,4,2,16,256]{4,3,2,1,0:T(8,128)} %get-tuple-element.14.meta), custom_call_target="tpu_custom_call" | custom-call | tf_op jit(solution)/shard_map/combine/pallas_call | solution.py:432
  448.8 2.3 copy.34
  (7 shorter events, 0.1 us)
Async XLA Ops:
  0.0 1.5 copy-start

commit v4 on v3

v4 whole, which is shorter than its diff:
```python
import functools

import jax
import jax.numpy as jnp
from jax import lax
from jax.experimental import pallas as pl
from jax.experimental.pallas import tpu as pltpu
from jax.sharding import PartitionSpec as P

MESH = pl.DeviceIdType.MESH
F32 = jnp.float32
BF16 = jnp.bfloat16
N = 4


def _cols(d):
    t = d // 128
    w = [(t // 3) * 128, (t // 3) * 128, (t - 2 * (t // 3)) * 128]
    return [(0, w[0]), (w[0], w[1]), (w[0] + w[1], w[2])]


def _where():
    o, e = lax.axis_index('outer'), lax.axis_index('expert')
    return o // N, o % N, e // 2, e % 2


def _dev(z, y, x, c):
    return (0, z * N + y, x * 2 + c)


def _along(p, me, a):
    z, y, x, c = me
    return _dev(*((a, y, x, c), (z, a, x, c), (z, y, a, c))[p])


def _plane(p, me, b, d, c):
    z, y, x, _ = me
    return _dev(*((z, b, d, c), (b, y, d, c), (b, d, x, c))[p])


def _copy(src, dst, send, recv, dev):
    return pltpu.make_async_remote_copy(src_ref=src, dst_ref=dst, send_sem=send, recv_sem=recv, device_id=dev, device_id_type=MESH)


def _wait(ref, sem):
    pltpu.make_async_copy(ref, ref, sem).wait()


def _hops(o):
    return o - 2 * (o // 3)


def _step(o, s):
    return (o + N - s * (o // 2) * (1 - o // 3)) % N


def _order(p, a, b, d):
    return ((a, b, d), (d, a, b), (b, d, a))[p]


def _dispatch(cols, x_ref, rows_ref, meta_ref, xin, meta_out, ag0, ag1, ag2, mt, mb, sb0, sb1, sb2, rl0, rl1, rl2,
              own, lown, asend, arecv, bsend, brecv, tsend, trecv, msend, mrecv, lsend, send, fsend, rrecv, recv):
    me = _where()
    z, y, x, c = me
    ag, sb, rl = (ag0, ag1, ag2), (sb0, sb1, sb2), (rl0, rl1, rl2)
    T = x_ref.shape[0]
    C = sb0.shape[3]
    L = 2 * N * C
    h = T // 2
    axis = (z, y, x)
    base = ((z, y, x), (y, x, z), (x, z, y))
    which = (0, 0, 1)
    parts = range(3)
    sides = (1, 3)
    halves = (pl.ds(0, h), pl.ds(h, h))

    def to_a(p, k):
        a, b, d = base[p]
        return _dev(*_order(p, (a + k) % N, b, d), c)

    def to_b(p, k):
        a, b, d = base[p]
        return _dev(*_order(p, a, (b + k) % N, d), c)

    def give_b(p, k, src):
        a, b, d = base[p]
        for q in range(2):
            _copy(src, ag[p].at[(a + k) % N, b], bsend.at[p, q, k], brecv.at[p, q, k], to_b(p, sides[q])).start()

    def pass_b(p, k):
        a, b, d = base[p]
        for q in range(2):
            _wait(ag[p].at[0, 0], brecv.at[p, q, k])
            blk = ag[p].at[(a + k) % N, (b + (3, 1)[q]) % N, halves[q]]
            _copy(blk, blk, bsend.at[p, 2 + q, k], brecv.at[p, 2 + q, k], to_b(p, sides[q])).start()

    for p in parts:
        a, b, d = base[p]
        blk = x_ref.at[:, pl.ds(*cols[p])]
        for q in range(2):
            _copy(blk, ag[p].at[a, b], asend.at[p, q], arecv.at[p, q], to_a(p, sides[q])).start()
        pltpu.make_async_copy(blk, ag[p].at[a, b], lown.at[p, 0]).start()
    for p in parts:
        a, b, d = base[p]
        for ka in range(N):
            for kb in range(N):
                at = _dev(*_order(p, (a + ka) % N, (b + kb) % N, d), c)
                src = rows_ref.at[p, (a + ka) % N * N + (b + kb) % N]
                if ka + kb:
                    _copy(src, mt.at[p, a, b], tsend.at[p], trecv.at[p], at).start()
                else:
                    pltpu.make_async_copy(src, mt.at[p, a, b], lown.at[p, 1]).start()
    for p in parts:
        give_b(p, 0, x_ref.at[:, pl.ds(*cols[p])])
    for p in parts:
        a, b, d = base[p]
        for q in range(2):
            _wait(ag[p].at[0, 0], arecv.at[p, q])
            blk = ag[p].at[(a + (3, 1)[q]) % N, b, halves[q]]
            _copy(blk, blk, asend.at[p, 2 + q], arecv.at[p, 2 + q], to_a(p, sides[q])).start()
    for p in parts:
        a, b, d = base[p]
        for k in sides:
            give_b(p, k, ag[p].at[(a + k) % N, b])
    for p in parts:
        for k in (1, 3, 2):
            _copy(meta_ref.at[which[p]], mb.at[p, axis[p]], msend.at[p, k], mrecv.at[p, k], _along(p, me, (axis[p] + k) % N)).start()
        pltpu.make_async_copy(meta_ref.at[which[p]], mb.at[p, axis[p]], lown.at[p, 2]).start()
    for p in parts:
        pass_b(p, 0)
    for p in parts:
        a, b, d = base[p]
        for q in range(2):
            _wait(ag[p].at[0, 0, halves[q]], arecv.at[p, 2 + q])
        give_b(p, 2, ag[p].at[(a + 2) % N, b])
        _wait(ag[p].at[0, 0], lown.at[p, 0])
        _wait(mt.at[p, 0, 0], lown.at[p, 1])
        _wait(rows_ref.at[p, pl.ds(0, N * N - 1)], trecv.at[p])

    def final(p, bs, ds):
        i = _order(p, slice(None), bs, ds)
        return xin.at[i[0], i[1], i[2], c, :, pl.ds(*cols[p])]

    def select(p, bo):
        a_, b, d = base[p]
        w = cols[p][1]
        bs = (b + bo) % N

        @pl.loop(0, N)
        def _(a):
            hot = lax.broadcasted_iota(jnp.int32, (T, L), 0).astype(F32) == mt[p, a, bs, 0:1, :]
            hot = jnp.where(hot, 1.0, 0.0).astype(BF16)
            r = lax.dot_general(hot, ag[p][a, bs], (((0,), (0,)), ((), ())), preferred_element_type=F32)
            sb[p][a, bo] = r.astype(BF16).reshape(2 * N, C, w)

        for do in (2, 1, 3, 0):
            for cc in range(2):
                s = 1 - 2 * cc
                src = sb[p].at[:, bo, (d + do) % N * 2 + (c + cc) % 2]
                if do == 2:
                    to = _dev(*_order(p, a_, b, (d + N + s) % N), c)
                    _copy(src, rl[p].at[bo, cc], lsend.at[p], rrecv.at[p, bo, cc], to).start()
                elif do + cc:
                    to = _dev(*_order(p, a_, b, (d + do) % N), (c + cc) % 2)
                    _copy(src, final(p, bs, d), send.at[p], recv.at[p], to).start()
                else:
                    pltpu.make_async_copy(src, final(p, bs, d), own.at[p]).start()

    def relay(p, bo):
        a, b, d = base[p]
        for cc in range(2):
            s = 1 - 2 * cc
            _wait(rl[p].at[bo, cc], rrecv.at[p, bo, cc])
            to = _dev(*_order(p, a, b, (d + N + s) % N), (c + cc) % 2)
            _copy(rl[p].at[bo, cc], final(p, (b + bo) % N, (d + N - s) % N), fsend.at[p], recv.at[p], to).start()

    for p in parts:
        select(p, 0)
        for k in sides:
            pass_b(p, k)
    for p in parts:
        pass_b(p, 2)
        for bo in sides:
            select(p, bo)
        relay(p, 0)
    for p in parts:
        for k in range(N):
            for q in range(2):
                _wait(ag[p].at[0, 0, halves[q]], brecv.at[p, 2 + q, k])
        select(p, 2)
        for bo in sides:
            relay(p, bo)
    for p in parts:
        relay(p, 2)
    for p in parts:
        _wait(mb.at[p, 0], lown.at[p, 2])
        for k in (1, 2, 3):
            _wait(mb.at[p, 0], mrecv.at[p, k])
    meta_out[...] = mb[...]
    for p in parts:
        for k in (1, 2, 3):
            _wait(mb.at[p, 0], msend.at[p, k])
        _wait(rows_ref.at[p, pl.ds(0, N * N - 1)], tsend.at[p])
        for q in range(2):
            _wait(ag[p].at[0, 0], asend.at[p, q])
            _wait(ag[p].at[0, 0, halves[q]], asend.at[p, 2 + q])
            for k in range(N):
                _wait(ag[p].at[0, 0], bsend.at[p, q, k])
                _wait(ag[p].at[0, 0, halves[q]], bsend.at[p, 2 + q, k])
        _wait(sb[p].at[:, :, 0], own.at[p])
        _wait(sb[p].at[:, :, pl.ds(0, 2)], fsend.at[p])
        _wait(sb[p].at[:, :, pl.ds(0, 2)], lsend.at[p])
        _wait(sb[p].at[:, :, pl.ds(0, 5)], send.at[p])
        _wait(sb[p].at[:, :, pl.ds(0, 7)], recv.at[p])


FIRST_B = (False, True, False)


def _bd(p, f, g):
    return (f, g) if FIRST_B[p] else (g, f)


def _spot(fo, go, cc, r):
    s = 1 - 2 * cc
    nf = min(r, _hops(fo))
    ng = r - nf
    return (N + {0: 0, 1: 1, 2: s, 3: -1}[fo] * nf) % N, (N + {0: 0, 1: 1, 2: s, 3: -1}[go] * ng) % N


WAYS = [(fo, go, cc) for fo in (2, 1, 3, 0) for go in (2, 1, 3, 0) for cc in range(2)]
LATER = [(k, r) for r in (2, 3) for k in WAYS if _hops(k[0]) + _hops(k[1]) > r]
ONCE = [k for k in WAYS if _hops(k[0]) + _hops(k[1]) > 1]
NEAR = 2 * N * N - len(ONCE) - 1


def _experts(cols, xin, w1_ref, w3_ref, w2_ref, r0, r1, r2, w1, w3, w2, xb, hb, ob, rl0, rl1, rl2, rm0, rm1, rm2,
             wsem, xsem, own, lsend, send, fsend, isend, rrecv, irecv, recv):
    me = _where()
    z, y, x, c = me
    R, rl, rm = (r0, r1, r2), (rl0, rl1, rl2), (rm0, rm1, rm2)
    C, D = xin.shape[4:]
    G = 2 * N * C
    ff = w1.shape[1]
    half = N // 2
    steps = N * half
    base = ((y, x), (z, x), (z, y))
    loads = [pltpu.make_async_copy(s.at[0], d, wsem.at[q]) for q, (s, d) in enumerate(((w1_ref, w1), (w3_ref, w3), (w2_ref, w2)))]

    def place(s):
        zo = (2 + 3 * (s // half)) % N
        yo = [(2 + 2 * (s % half) + 3 * q) % N for q in range(2)]
        return (z + zo) % N, zo, [(y + o) % N for o in yo], yo

    def load(s):
        zt, _, ys, _ = place(s)
        return [pltpu.make_async_copy(xin.at[zt, yv], xb.at[s % 2, q], xsem.at[s % 2, q]) for q, yv in enumerate(ys)]

    for q in load(0):
        q.start()
    for q in loads:
        q.start()
    cs = [pl.ds(lo, w) for lo, w in cols]

    def at(p, f, g, cc):
        bo, do = _bd(p, f, g)
        return _plane(p, me, (base[p][0] + bo) % N, (base[p][1] + do) % N, (c + cc) % 2)

    def put(p, src, fo, go, cc, lead):
        s = 1 - 2 * cc
        key = (fo * N + go) * 2 + cc
        n = _hops(fo) + _hops(go)
        hf, hg = _step(fo, s), (1 - (fo + N - 1) // N) * _step(go, s)
        dst = R[p].at[lead, (base[p][0] * N + base[p][1]) * 2 + c]
        leg = _copy(src, rl[p].at[lead, key], lsend.at[p], rrecv.at[p, key], at(p, hf, hg, 0))
        far = _copy(src, dst, send.at[p], recv.at[p], at(p, hf, hg, cc))

        @pl.when(n > 1)
        def _():
            leg.start()

        if cc:
            @pl.when(n < 2)
            def _():
                far.start()
        else:
            @pl.when(n == 1)
            def _():
                far.start()

            @pl.when(n == 0)
            def _():
                pltpu.make_async_copy(src, dst, own.at[p]).start()

    fs, ds = min(256, ff), min(512, D)
    every = slice(None)

    @pl.loop(0, steps)
    def _(s):
        zt, zo, ys, yo = place(s)
        jp = s % half

        @pl.when(s + 1 < steps)
        def _():
            for q in load(s + 1):
                q.start()

        for q in load(s):
            q.wait()

        @pl.when(s == 0)
        def _():
            for q in loads:
                q.wait()

        @pl.loop(0, ff // fs)
        def _(f):
            fc = pl.ds(pl.multiple_of(f * fs, fs), fs)
            xt = xb[s % 2].reshape(2 * G, D)
            a = jnp.dot(xt, w1[:, fc], preferred_element_type=F32)
            b = jnp.dot(xt, w3[:, fc], preferred_element_type=F32)
            hb[:, fc] = (jax.nn.silu(a) * b).astype(BF16)

        @pl.loop(0, D // ds)
        def _(f):
            fc = pl.ds(pl.multiple_of(f * ds, ds), ds)
            o = jnp.dot(hb[...], w2[:, fc], preferred_element_type=F32).astype(BF16)
            ob[zt, ys[0], :, :, :, fc] = o[:G].reshape(N, 2, C, ds)
            ob[zt, ys[1], :, :, :, fc] = o[G:].reshape(N, 2, C, ds)

        for q in range(2):
            for cc in range(2):
                put(2, ob.at[zt, ys[q], :, (c + cc) % 2, :, cs[2]], yo[q], zo, cc, every)

            @pl.loop(0, N)
            def _(j):
                do = (2 + 3 * j) % N
                for cc in range(2):
                    put(0, ob.at[zt, ys[q], (x + do) % N, (c + cc) % 2, :, cs[0]], do, yo[q], cc, zt)

        @pl.when(jp == half - 1)
        def _():
            @pl.loop(0, N)
            def _(j):
                do = (2 + 3 * j) % N
                for cc in range(2):
                    put(1, ob.at[zt, :, (x + do) % N, (c + cc) % 2, :, cs[1]], zo, do, cc, every)

    def forward(p, key, r):
        fo, go, cc = key
        here, there = _spot(fo, go, cc, r), _spot(fo, go, cc, r + 1)
        k = (fo * N + go) * 2 + cc
        if r == 1:
            buf, sem = rl[p].at[:, k], rrecv.at[p, k]
        else:
            k = LATER.index((key, r))
            buf, sem = rm[p].at[:, k], irecv.at[p, k]
        _wait(buf, sem)
        hop = [(there[q] + N - here[q]) % N for q in range(2)]
        if r + 1 == _hops(fo) + _hops(go):
            bs, ds = ((base[p][q] + N - v) % N for q, v in enumerate(_bd(p, *here)))
            _copy(buf, R[p].at[:, (bs * N + ds) * 2 + c], fsend.at[p], recv.at[p], at(p, *hop, cc)).start()
        else:
            k = LATER.index((key, r + 1))
            _copy(buf, rm[p].at[:, k], isend.at[p], irecv.at[p, k], at(p, *hop, 0)).start()

    for long in (True, False):
        for key in ONCE:
            if (_hops(key[0]) + _hops(key[1]) > 2) == long:
                for p in (2, 1, 0):
                    forward(p, key, 1)
    for key, r in LATER:
        for p in (2, 1, 0):
            forward(p, key, r)
    for p in range(3):
        _wait(R[p].at[:, 0], own.at[p])
        _wait(R[p].at[:, pl.ds(0, NEAR)], send.at[p])
        _wait(R[p].at[:, pl.ds(0, len(ONCE))], lsend.at[p])
        _wait(R[p].at[:, pl.ds(0, len(ONCE))], fsend.at[p])
        _wait(R[p].at[:, pl.ds(0, len(LATER))], isend.at[p])
        _wait(R[p].at[:, pl.ds(0, 2 * N * N - 1)], recv.at[p])


def _combine(cols, r0, r1, r2, meta, y_ref, b0, b1, b2, p0, p1, p2, q0, q1, q2, h0, h1, h2, mw, rsem, send, recv):
    me = _where()
    z, y, x, c = me
    R, B, S, Q, H = (r0, r1, r2), (b0, b1, b2), (p0, p1, p2), (q0, q1, q2), (h0, h1, h2)
    axis = (z, y, x)
    T = y_ref.shape[0]
    C = b0.shape[2]
    L = 2 * N * C
    h = T // 2
    halves = (pl.ds(0, h), pl.ds(h, h))
    for p in range(3):
        for k in (2, 1, 3, 0):
            a = (axis[p] + k) % N
            pltpu.make_async_copy(R[p].at[a], B[p].at[a], rsem.at[p, k]).start()

    def partial(p, k):
        a = (axis[p] + k) % N
        _wait(B[p].at[0], rsem.at[p, k])

        @pl.loop(0, N)
        def _(b):
            row = (z * N + b, b * N + y, b * N + x)[p]
            tab = meta[p, a, 0, pl.ds(row, 1), :]
            g = meta[p, a, 1, pl.ds(row, 1), :]
            hot = lax.broadcasted_iota(jnp.int32, (T, L), 0).astype(F32) == tab
            m = jnp.where(hot, g, 0.0)
            here = pl.ds(pl.multiple_of(b * L, L), L)
            for q in range(3):
                part = m.astype(BF16)
                mw[q * T:(q + 1) * T, here] = part
                m = m - part.astype(F32)

        v = B[p][a].reshape(N * L, cols[p][1])
        t = jnp.dot(mw[...], v, preferred_element_type=F32)
        S[p][k] = t[:T] + t[T:2 * T] + t[2 * T:]

    def side(p, k):
        return _along(p, me, (axis[p] + (1, 3)[k]) % N)

    for p in range(3):
        partial(p, 2)
        for k in range(2):
            _copy(S[p].at[2, halves[k]], H[p].at[k], send.at[p, k], recv.at[p, k], side(p, k)).start()
    for p in range(3):
        for k in range(2):
            partial(p, (1, 3)[k])
            _wait(H[p].at[k], recv.at[p, k])
            S[p][(1, 3)[k], halves[k]] += H[p][k]
            _copy(S[p].at[(1, 3)[k]], Q[p].at[k], send.at[p, 2 + k], recv.at[p, 2 + k], side(p, k)).start()
    for p in range(3):
        partial(p, 0)
    for p in range(3):
        t = S[p][0]
        for k in range(2):
            _wait(Q[p].at[k], recv.at[p, 2 + k])
            t += Q[p][k]
        y_ref[:, pl.ds(*cols[p])] = t.astype(BF16)
    for p in range(3):
        for k in range(2):
            _wait(H[p].at[k], send.at[p, k])
            _wait(Q[p].at[k], send.at[p, 2 + k])


def _plan(x, wr, idx, cap):
    T = x.shape[0]
    E = wr.shape[1]
    logits = jnp.dot(x, wr, preferred_element_type=F32)
    oh = idx[:, :, None] == jnp.arange(E, dtype=idx.dtype)
    g = jax.nn.softmax(jnp.sum(jnp.where(oh, logits[:, None, :], 0.0), axis=-1), axis=-1)
    m = jnp.sum(oh, axis=1, dtype=jnp.int32).astype(F32)
    ge = jnp.sum(jnp.where(oh, g[:, :, None], 0.0), axis=1)
    pos = jnp.arange(T, dtype=jnp.int32)
    tri = (pos[None, :] < pos[:, None]).astype(BF16)
    cnt = jnp.dot(tri, m.astype(BF16), preferred_element_type=F32)
    cnt = jnp.where(m > 0, cnt, -1.0)
    hit = cnt[:, :, None] == jnp.arange(cap, dtype=F32)
    tab = jnp.sum(jnp.where(hit, pos.astype(F32)[:, None, None] + 1.0, 0.0), axis=0) - 1.0
    gw = jnp.sum(jnp.where(hit, ge[:, :, None], 0.0), axis=0)

    def both(v):
        v = v.reshape(N, N, N, 2 * cap)
        return v.reshape(N * N, 2 * N * cap), v.transpose(0, 2, 1, 3).reshape(N * N, 2 * N * cap)

    (t0, t2), (g0, g2) = both(tab), both(gw)
    t = tab.reshape(N, N, N, 2 * cap)
    rows = jnp.stack([t, t.transpose(1, 2, 0, 3), t.transpose(2, 0, 1, 3)]).reshape(3, N * N, 1, 2 * N * cap)
    return jnp.broadcast_to(rows, (3, N * N, 8, 2 * N * cap)), jnp.stack([jnp.stack([t0, g0]), jnp.stack([t2, g2])])


def solution(mesh):
    assert (mesh.shape['outer'], mesh.shape['expert']) == (N * N, 2 * N)
    tok = P(('data', 'outer', 'expert'), None)
    wsp = P(('outer', 'expert'), None, None)
    any_ = pl.BlockSpec(memory_space=pl.ANY)
    vmem = pl.BlockSpec(memory_space=pltpu.VMEM)
    dma = pltpu.SemaphoreType.DMA
    params = pltpu.CompilerParams(has_side_effects=True, vmem_limit_bytes=63 * 1024 * 1024)

    def local(x, wr, idx, w1, w3, w2):
        T, D = x.shape
        E = wr.shape[1]
        C = 2 * T * idx.shape[1] // E
        ff = w1.shape[2]
        cols = _cols(D)
        widths = [w for _, w in cols]
        L = 2 * N * C
        K = 2 * N * N
        blocks = [(N, K, C, w) for w in widths]
        held = [pltpu.VMEM(b, BF16) for b in blocks]
        rows, meta = _plan(x, wr, idx, C)
        xin, metas = pl.pallas_call(
            functools.partial(_dispatch, cols),
            name='dispatch',
            out_shape=[jax.ShapeDtypeStruct((N, N, N, 2, C, D), BF16), jax.ShapeDtypeStruct((3, N, 2, N * N, L), F32)],
            in_specs=[any_] * 3,
            out_specs=[any_, vmem],
            scratch_shapes=[pltpu.VMEM((N, N, T, w), BF16) for w in widths]
            + [pltpu.VMEM((3, N, N, 8, L), F32), pltpu.VMEM((3, N, 2, N * N, L), F32)]
            + [pltpu.VMEM((N, N, 2 * N, C, w), BF16) for w in widths] + [pltpu.VMEM((N, 2, N, C, w), BF16) for w in widths]
            + [dma((3,)), dma((3, 3)), dma((3, 4)), dma((3, 4)), dma((3, 4, N)), dma((3, 4, N)), dma((3,)), dma((3,)), dma((3, 4)), dma((3, 4)),
               dma((3,)), dma((3,)), dma((3,)), dma((3, N, 2)), dma((3,))],
            compiler_params=params,
        )(x, rows, meta)
        r = pl.pallas_call(
            functools.partial(_experts, cols),
            name='experts',
            out_shape=[jax.ShapeDtypeStruct(b, BF16) for b in blocks],
            in_specs=[any_] * 4,
            out_specs=[any_] * 3,
            scratch_shapes=[
                pltpu.VMEM((D, ff), BF16), pltpu.VMEM((D, ff), BF16), pltpu.VMEM((ff, D), BF16),
                pltpu.VMEM((2, 2, N, 2, C, D), BF16), pltpu.VMEM((2 * L, ff), BF16), pltpu.VMEM((N, N, N, 2, C, D), BF16), *held,
                *(pltpu.VMEM((N, len(LATER), C, w), BF16) for w in widths),
                dma((3,)), dma((2, 2)), dma((3,)), dma((3,)), dma((3,)), dma((3,)), dma((3,)), dma((3, K)), dma((3, len(LATER))), dma((3,)),
            ],
            compiler_params=params,
        )(xin, w1, w3, w2)
        return pl.pallas_call(
            functools.partial(_combine, cols),
            name='combine',
            out_shape=jax.ShapeDtypeStruct((T, D), BF16),
            in_specs=[any_] * 3 + [vmem],
            out_specs=vmem,
            scratch_shapes=held + [pltpu.VMEM((N, T, w), F32) for w in widths] + [pltpu.VMEM((2, T, w), F32) for w in widths]
            + [pltpu.VMEM((2, T // 2, w), F32) for w in widths] + [pltpu.VMEM((3 * T, N * L), BF16), dma((3, N)), dma((3, 4)), dma((3, 4))],
            compiler_params=params,
        )(*r, metas)

    return jax.shard_map(local, mesh=mesh, in_specs=(tok, P(None, None), tok, wsp, wsp, wsp), out_specs=tok, check_vma=False)
```

time: 451 us -> 388 us (0.86)
  Pallas kernels: 441 us -> 377 us
    pallas_call x1, Pallas kernels: 186 us -> 147 us  [local(): pl.pallas_call(functools.partial(_dispatch, cols), name='dispatch', out_s...]
    pallas_call x1, Pallas kernels: 199 us -> 175 us  [local(): pl.pallas_call(functools.partial(_experts, cols), name='experts', out_sha...]
where the time goes in v4:
time: 388 us
  Pallas kernels  377 us (97%)
  local copies, waits for them, and re-layouts  5.16 us (1%)
  other arithmetic  4 us (1%)
    pallas_call x1, Pallas kernels, local(): pl.pallas_call(functools.partial(_experts, cols), name='experts', out_sha...  175 us
    pallas_call x1, Pallas kernels, local(): pl.pallas_call(functools.partial(_dispatch, cols), name='dispatch', out_s...  147 us
    pallas_call x1, Pallas kernels, local(): pl.pallas_call(functools.partial(_combine, cols), name='combine', out_sha...  55.4 us

profile of v4, /device:TPU:0, one launch (start us, length us, event | category | flops | bytes accessed | tf_op | source)
XLA Modules:
  0.0 388.3 jit_solution(344181044237201656)
XLA Ops:
  0.0 0.0 copy-start
  0.0 0.9 copy.28
  0.9 0.4 convert_reduce_fusion
  1.3 0.2 convolution_select_fusion
  1.5 0.0 copy-done
  1.5 1.7 fusion.2
  3.1 0.9 select_reduce_fusion.3
  4.0 0.1 reduce_max.9
  4.1 0.1 copy.35
  4.3 0.1 copy.36
  4.4 1.3 select_reduce_fusion.2
  5.7 0.7 select_reduce_fusion
  6.4 0.1 copy.29
  6.5 0.1 sub.25
  6.6 0.1 sub.23
  6.6 0.1 sub.24
  6.8 0.1 stack.24
  6.9 0.1 stack.25
  7.0 0.1 stack_reshape.7
  7.1 0.1 copy.37
  7.2 0.1 stack_reshape_reshape.4
  7.2 0.1 reshape.84
  7.3 0.1 stack_reshape.8
  7.4 0.6 pad_maximum_fusion.meta_ref
  8.1 0.8 broadcast_in_dim.71.rows_ref
  8.8 146.9 %dispatch.1 = (bf16[4,4,4,2,32,2048]{5,4,3,2,1,0:T(8,128)(2,1)}, f32[3,4,2,16,256]{4,3,2,1,0:T(8,128)}) custom-call(bf16[256,2048]{1,0:T(8,128)(2,1)} %x_ref.1, f32[3,16,8,256]{3,2,1,0:T(8,128)} %broadcast_in_dim.71.rows_ref, f32[2,2,16,256]{3,2,1,0:T(8,128)} %pad_maximum_fusion.meta_ref), custom_call_target="tpu_custom_call" | custom-call | tf_op jit(solution)/shard_map/dispatch/pallas_call | solution.py:494
  155.8 174.7 %experts.1 = (bf16[4,32,32,640]{3,2,1,0:T(8,128)(2,1)}, bf16[4,32,32,640]{3,2,1,0:T(8,128)(2,1)}, bf16[4,32,32,768]{3,2,1,0:T(8,128)(2,1)}) custom-call(bf16[4,4,4,2,32,2048]{5,4,3,2,1,0:T(8,128)(2,1)} %get-tuple-element.10.xin, bf16[1,2048,768]{2,1,0:T(8,128)(2,1)} %w1_ref.1, bf16[1,2048,768]{2,1,0:T(8,128)(2,1)} %w3_ref.1, bf16[1,768,2048]{2,1,0:T(8,128)(2,1)} %w2_ref.1), custom_call_target="tpu_custom_call" | custom-call | tf_op jit(solution)/shard_map/experts/pallas_call | solution.py:507
  330.5 55.4 %combine.1 = bf16[256,2048]{1,0:T(8,128)(2,1)} custom-call(bf16[4,32,32,640]{3,2,1,0:T(8,128)(2,1)} %get-tuple-element.11.r0, bf16[4,32,32,640]{3,2,1,0:T(8,128)(2,1)} %get-tuple-element.12.r1, bf16[4,32,32,768]{3,2,1,0:T(8,128)(2,1)} %get-tuple-element.13.r2, f32[3,4,2,16,256]{4,3,2,1,0:T(8,128)} %get-tuple-element.14.meta), custom_call_target="tpu_custom_call" | custom-call | tf_op jit(solution)/shard_map/combine/pallas_call | solution.py:521
  386.0 2.3 copy.43
  (10 shorter events, 0.1 us)
Async XLA Ops:
  0.0 1.5 copy-start

commit v5 on v4

--- a/solution.py
+++ b/solution.py
@@ -233,31 +233,70 @@
 ONCE = [k for k in WAYS if _hops(k[0]) + _hops(k[1]) > 1]
 NEAR = 2 * N * N - len(ONCE) - 1
 
-
-def _experts(cols, xin, w1_ref, w3_ref, w2_ref, r0, r1, r2, w1, w3, w2, xb, hb, ob, rl0, rl1, rl2, rm0, rm1, rm2,
-             wsem, xsem, own, lsend, send, fsend, isend, rrecv, irecv, recv):
+TILES = [((2, 2), (2, 1)), ((2, 3), (2, 0)), ((1, 2), (3, 2)), ((0, 2), (1, 1)),
+         ((1, 3), (1, 0)), ((3, 1), (0, 1)), ((3, 3), (3, 0)), ((0, 3), (0, 0))]
+LAG = 2
+
+
+def _messages():
+    seen, steps = set(), []
+    for tile in TILES:
+        out = []
+        for zo, yo in tile:
+            seen.add((zo, yo))
+            for cc in range(2):
+                out.append((2, yo, zo, cc))
+        for o in dict.fromkeys(v[0] for v in tile):
+            if all((o, k) in seen for k in range(N)) and not any(m[0] == 1 and m[1] == o for t in steps for m in t):
+                out += [(1, o, do, cc) for do in (2, 1, 3, 0) for cc in range(2)]
+        for o in dict.fromkeys(v[1] for v in tile):
+            if all((k, o) in seen for k in range(N)) and not any(m[0] == 0 and m[2] == o for t in steps for m in t):
+                out += [(0, do, o, cc) for do in (2, 1, 3, 0) for cc in range(2)]
+        steps.append(out)
+    assert sum(len(t) for t in steps) == 3 * len(WAYS)
+    return steps
+
+
+def _schedule():
+    first = _messages()
+    left = {}
+    for st, out in enumerate(first):
+        for m in out:
+            n = _hops(m[1]) + _hops(m[2])
+            for r in range(1, n):
+                left.setdefault(min(st + LAG * r, len(TILES)), []).append((r, (m[0], m[1:], r)))
+    return first, [[v for _, v in sorted(left.get(st, []), key=lambda t: t[0])] for st in range(len(TILES) + 1)]
+
+
+def _pick(values, s):
+    return sum(v * (1 - ((s - k) * (s - k) + 63) // 64) for k, v in enumerate(values))
+
+
+def _experts(cols, xin, w1_ref, w3_ref, w2_ref, meta, y_ref, r0, r1, r2, rm0, rm1, rm2, w1, w3, w2, xb, hb, ob, rl0, rl1, rl2,
+             s0, s1, s2, q0, q1, q2, h0, h1, h2,
+             wsem, xsem, own, lsend, send, fsend, isend, rrecv, irecv, recv, bsem, ssend, srecv):
     me = _where()
     z, y, x, c = me
     R, rl, rm = (r0, r1, r2), (rl0, rl1, rl2), (rm0, rm1, rm2)
     C, D = xin.shape[4:]
     G = 2 * N * C
     ff = w1.shape[1]
-    half = N // 2
-    steps = N * half
+    steps = len(TILES)
     base = ((y, x), (z, x), (z, y))
+    axis = (z, y, x)
+    first, later = _schedule()
     loads = [pltpu.make_async_copy(s.at[0], d, wsem.at[q]) for q, (s, d) in enumerate(((w1_ref, w1), (w3_ref, w3), (w2_ref, w2)))]
 
-    def place(s):
-        zo = (2 + 3 * (s // half)) % N
-        yo = [(2 + 2 * (s % half) + 3 * q) % N for q in range(2)]
-        return (z + zo) % N, zo, [(y + o) % N for o in yo], yo
-
-    def load(s):
-        zt, _, ys, _ = place(s)
-        return [pltpu.make_async_copy(xin.at[zt, yv], xb.at[s % 2, q], xsem.at[s % 2, q]) for q, yv in enumerate(ys)]
-
-    for q in load(0):
-        q.start()
+    def cell(st, q):
+        zo, yo = TILES[st][q]
+        return (z + zo) % N, (y + yo) % N
+
+    def load(st):
+        for q in range(2):
+            zt, yv = cell(st, q)
+            pltpu.make_async_copy(xin.at[zt, yv], xb.at[st % 2, q], xsem.at[st % 2, q]).start()
+
+    load(0)
     for q in loads:
         q.start()
     cs = [pl.ds(lo, w) for lo, w in cols]
@@ -266,91 +305,27 @@
         bo, do = _bd(p, f, g)
         return _plane(p, me, (base[p][0] + bo) % N, (base[p][1] + do) % N, (c + cc) % 2)
 
-    def put(p, src, fo, go, cc, lead):
-        s = 1 - 2 * cc
-        key = (fo * N + go) * 2 + cc
+    def slot(p, b, d):
+        return R[p].at[:, pl.ds(((b * N + d) * 2 + c) * C, C)]
+
+    def put(p, fo, go, cc):
+        bo, do = _bd(p, fo, go)
+        b, d, c2 = (base[p][0] + bo) % N, (base[p][1] + do) % N, (c + cc) % 2
+        src = (ob.at[:, b, d, c2, :, cs[0]], ob.at[b, :, d, c2, :, cs[1]], ob.at[b, d, :, c2, :, cs[2]])[p]
         n = _hops(fo) + _hops(go)
-        hf, hg = _step(fo, s), (1 - (fo + N - 1) // N) * _step(go, s)
-        dst = R[p].at[lead, (base[p][0] * N + base[p][1]) * 2 + c]
-        leg = _copy(src, rl[p].at[lead, key], lsend.at[p], rrecv.at[p, key], at(p, hf, hg, 0))
-        far = _copy(src, dst, send.at[p], recv.at[p], at(p, hf, hg, cc))
-
-        @pl.when(n > 1)
-        def _():
-            leg.start()
-
-        if cc:
-            @pl.when(n < 2)
-            def _():
-                far.start()
+        if n > 1:
+            k = ONCE.index((fo, go, cc))
+            _copy(src, rl[p].at[:, k], lsend.at[p], rrecv.at[p, k], at(p, *_spot(fo, go, cc, 1), 0)).start()
+        elif n + cc:
+            _copy(src, slot(p, *base[p]), send.at[p], recv.at[p], _plane(p, me, b, d, c2)).start()
         else:
-            @pl.when(n == 1)
-            def _():
-                far.start()
-
-            @pl.when(n == 0)
-            def _():
-                pltpu.make_async_copy(src, dst, own.at[p]).start()
-
-    fs, ds = min(256, ff), min(512, D)
-    every = slice(None)
-
-    @pl.loop(0, steps)
-    def _(s):
-        zt, zo, ys, yo = place(s)
-        jp = s % half
-
-        @pl.when(s + 1 < steps)
-        def _():
-            for q in load(s + 1):
-                q.start()
-
-        for q in load(s):
-            q.wait()
-
-        @pl.when(s == 0)
-        def _():
-            for q in loads:
-                q.wait()
-
-        @pl.loop(0, ff // fs)
-        def _(f):
-            fc = pl.ds(pl.multiple_of(f * fs, fs), fs)
-            xt = xb[s % 2].reshape(2 * G, D)
-            a = jnp.dot(xt, w1[:, fc], preferred_element_type=F32)
-            b = jnp.dot(xt, w3[:, fc], preferred_element_type=F32)
-            hb[:, fc] = (jax.nn.silu(a) * b).astype(BF16)
-
-        @pl.loop(0, D // ds)
-        def _(f):
-            fc = pl.ds(pl.multiple_of(f * ds, ds), ds)
-            o = jnp.dot(hb[...], w2[:, fc], preferred_element_type=F32).astype(BF16)
-            ob[zt, ys[0], :, :, :, fc] = o[:G].reshape(N, 2, C, ds)
-            ob[zt, ys[1], :, :, :, fc] = o[G:].reshape(N, 2, C, ds)
-
-        for q in range(2):
-            for cc in range(2):
-                put(2, ob.at[zt, ys[q], :, (c + cc) % 2, :, cs[2]], yo[q], zo, cc, every)
-
-            @pl.loop(0, N)
-            def _(j):
-                do = (2 + 3 * j) % N
-                for cc in range(2):
-                    put(0, ob.at[zt, ys[q], (x + do) % N, (c + cc) % 2, :, cs[0]], do, yo[q], cc, zt)
-
-        @pl.when(jp == half - 1)
-        def _():
-            @pl.loop(0, N)
-            def _(j):
-                do = (2 + 3 * j) % N
-                for cc in range(2):
-                    put(1, ob.at[zt, :, (x + do) % N, (c + cc) % 2, :, cs[1]], zo, do, cc, every)
+            pltpu.make_async_copy(src, slot(p, *base[p]), own.at[p]).start()
 
     def forward(p, key, r):
         fo, go, cc = key
         here, there = _spot(fo, go, cc, r), _spot(fo, go, cc, r + 1)
-        k = (fo * N + go) * 2 + cc
         if r == 1:
+            k = ONCE.index(key)
             buf, sem = rl[p].at[:, k], rrecv.at[p, k]
         else:
             k = LATER.index((key, r))
@@ -359,46 +334,72 @@
         hop = [(there[q] + N - here[q]) % N for q in range(2)]
         if r + 1 == _hops(fo) + _hops(go):
             bs, ds = ((base[p][q] + N - v) % N for q, v in enumerate(_bd(p, *here)))
-            _copy(buf, R[p].at[:, (bs * N + ds) * 2 + c], fsend.at[p], recv.at[p], at(p, *hop, cc)).start()
+            _copy(buf, slot(p, bs, ds), fsend.at[p], recv.at[p], at(p, *hop, cc)).start()
         else:
             k = LATER.index((key, r + 1))
             _copy(buf, rm[p].at[:, k], isend.at[p], irecv.at[p, k], at(p, *hop, 0)).start()
 
-    for long in (True, False):
-        for key in ONCE:
-            if (_hops(key[0]) + _hops(key[1]) > 2) == long:
-                for p in (2, 1, 0):
-                    forward(p, key, 1)
-    for key, r in LATER:
-        for p in (2, 1, 0):
-            forward(p, key, r)
-    for p in range(3):
-        _wait(R[p].at[:, 0], own.at[p])
-        _wait(R[p].at[:, pl.ds(0, NEAR)], send.at[p])
-        _wait(R[p].at[:, pl.ds(0, len(ONCE))], lsend.at[p])
-        _wait(R[p].at[:, pl.ds(0, len(ONCE))], fsend.at[p])
-        _wait(R[p].at[:, pl.ds(0, len(LATER))], isend.at[p])
-        _wait(R[p].at[:, pl.ds(0, 2 * N * N - 1)], recv.at[p])
-
-
-def _combine(cols, r0, r1, r2, meta, y_ref, b0, b1, b2, p0, p1, p2, q0, q1, q2, h0, h1, h2, mw, rsem, send, recv):
-    me = _where()
-    z, y, x, c = me
-    R, B, S, Q, H = (r0, r1, r2), (b0, b1, b2), (p0, p1, p2), (q0, q1, q2), (h0, h1, h2)
-    axis = (z, y, x)
+    fs, ds = min(256, ff), min(512, D)
+
+    @pl.loop(0, steps)
+    def _(s):
+        zt = [(z + _pick([t[q][0] for t in TILES], s)) % N for q in range(2)]
+        yt = [(y + _pick([t[q][1] for t in TILES], s)) % N for q in range(2)]
+        for st in range(steps - 1):
+            @pl.when(s == st)
+            def _():
+                load(st + 1)
+
+        for q in range(2):
+            _wait(xb.at[0, q], xsem.at[s % 2, q])
+
+        @pl.when(s == 0)
+        def _():
+            for q in loads:
+                q.wait()
+
+        @pl.loop(0, ff // fs)
+        def _(f):
+            fc = pl.ds(pl.multiple_of(f * fs, fs), fs)
+            xt = xb[s % 2].reshape(2 * G, D)
+            a = jnp.dot(xt, w1[:, fc], preferred_element_type=F32)
+            b = jnp.dot(xt, w3[:, fc], preferred_element_type=F32)
+            hb[:, fc] = (jax.nn.silu(a) * b).astype(BF16)
+
+        @pl.loop(0, D // ds)
+        def _(f):
+            fc = pl.ds(pl.multiple_of(f * ds, ds), ds)
+            o = jnp.dot(hb[...], w2[:, fc], preferred_element_type=F32).astype(BF16)
+            ob[zt[0], yt[0], :, :, :, fc] = o[:G].reshape(N, 2, C, ds)
+            ob[zt[1], yt[1], :, :, :, fc] = o[G:].reshape(N, 2, C, ds)
+
+        for st in range(steps):
+            @pl.when(s == st)
+            def _():
+                for m in first[st]:
+                    put(*m)
+                for v in later[st]:
+                    forward(*v)
+
+    S, Q, H = (s0, s1, s2), (q0, q1, q2), (h0, h1, h2)
     T = y_ref.shape[0]
-    C = b0.shape[2]
     L = 2 * N * C
     h = T // 2
     halves = (pl.ds(0, h), pl.ds(h, h))
-    for p in range(3):
+    sides = (1, 3)
+
+    def room(k, p):
+        return (w1, w3)[k // 2].at[pl.ds(k % 2 * N * L, N * L), pl.ds(0, cols[p][1])]
+
+    def gather(p):
+        _wait(slot(p, 0, 0), own.at[p])
+        _wait(R[p].at[:, pl.ds(0, (2 * N * N - 1) * C)], recv.at[p])
         for k in (2, 1, 3, 0):
-            a = (axis[p] + k) % N
-            pltpu.make_async_copy(R[p].at[a], B[p].at[a], rsem.at[p, k]).start()
+            pltpu.make_async_copy(R[p].at[(axis[p] + k) % N], room(k, p), bsem.at[k]).start()
 
     def partial(p, k):
         a = (axis[p] + k) % N
-        _wait(B[p].at[0], rsem.at[p, k])
+        _wait(room(k, p), bsem.at[k])
 
         @pl.loop(0, N)
         def _(b):
@@ -410,38 +411,65 @@
             here = pl.ds(pl.multiple_of(b * L, L), L)
             for q in range(3):
                 part = m.astype(BF16)
-                mw[q * T:(q + 1) * T, here] = part
+                w2[q * T:(q + 1) * T, here] = part
                 m = m - part.astype(F32)
 
-        v = B[p][a].reshape(N * L, cols[p][1])
-        t = jnp.dot(mw[...], v, preferred_element_type=F32)
+        t = jnp.dot(w2[:, pl.ds(0, N * L)], room(k, p)[...], preferred_element_type=F32)
         S[p][k] = t[:T] + t[T:2 * T] + t[2 * T:]
 
-    def side(p, k):
-        return _along(p, me, (axis[p] + (1, 3)[k]) % N)
-
+    def side(p, q):
+        return _along(p, me, (axis[p] + sides[q]) % N)
+
+    def halfway(p):
+        for q in range(2):
+            _copy(S[p].at[2, halves[q]], H[p].at[q], ssend.at[p, q], srecv.at[p, q], side(p, q)).start()
+
+    def onward(p):
+        for q in range(2):
+            _wait(H[p].at[q], srecv.at[p, q])
+            S[p][sides[q], halves[q]] += H[p][q]
+            _copy(S[p].at[sides[q]], Q[p].at[q], ssend.at[p, 2 + q], srecv.at[p, 2 + q], side(p, q)).start()
+
+    rest = later[steps]
+    for v in rest:
+        if v[0] == 2 or v[2] == 1:
+            forward(*v)
+    more = [v for v in rest if not (v[0] == 2 or v[2] == 1)]
+    gather(2)
+    partial(2, 2)
+    halfway(2)
+    for v in more:
+        if v[2] == 2:
+            forward(*v)
+    partial(2, 1)
+    for v in more:
+        if v[2] == 3:
+            forward(*v)
+    partial(2, 3)
+    onward(2)
+    partial(2, 0)
+    for p in (1, 0):
+        gather(p)
+        partial(p, 2)
+        halfway(p)
+        partial(p, 1)
+        partial(p, 3)
+        onward(p)
+        partial(p, 0)
+    for p in (2, 1, 0):
+        t = S[p][0]
+        for q in range(2):
+            _wait(Q[p].at[q], srecv.at[p, 2 + q])
+            t += Q[p][q]
+        y_ref[:, cs[p]] = t.astype(BF16)
     for p in range(3):
-        partial(p, 2)
-        for k in range(2):
-            _copy(S[p].at[2, halves[k]], H[p].at[k], send.at[p, k], recv.at[p, k], side(p, k)).start()
-    for p in range(3):
-        for k in range(2):
-            partial(p, (1, 3)[k])
-            _wait(H[p].at[k], recv.at[p, k])
-            S[p][(1, 3)[k], halves[k]] += H[p][k]
-            _copy(S[p].at[(1, 3)[k]], Q[p].at[k], send.at[p, 2 + k], recv.at[p, 2 + k], side(p, k)).start()
-    for p in range(3):
-        partial(p, 0)
-    for p in range(3):
-        t = S[p][0]
-        for k in range(2):
-            _wait(Q[p].at[k], recv.at[p, 2 + k])
-            t += Q[p][k]
-        y_ref[:, pl.ds(*cols[p])] = t.astype(BF16)
-    for p in range(3):
-        for k in range(2):
-            _wait(H[p].at[k], send.at[p, k])
-            _wait(Q[p].at[k], send.at[p, 2 + k])
+        for q in range(2):
+            _wait(H[p].at[q], ssend.at[p, q])
+            _wait(Q[p].at[q], ssend.at[p, 2 + q])
+        _wait(R[p].at[:, pl.ds(0, NEAR * C)], send.at[p])
+        _wait(R[p].at[:, pl.ds(0, len(ONCE) * C)], lsend.at[p])
+        _wait(R[p].at[:, pl.ds(0, len(ONCE) * C)], fsend.at[p])
+        _wait(R[p].at[:, pl.ds(0, len(LATER) * C)], isend.at[p])
 
 
 def _plan(x, wr, idx, cap):
@@ -477,7 +505,7 @@
     any_ = pl.BlockSpec(memory_space=pl.ANY)
     vmem = pl.BlockSpec(memory_space=pltpu.VMEM)
     dma = pltpu.SemaphoreType.DMA
-    params = pltpu.CompilerParams(has_side_effects=True, vmem_limit_bytes=63 * 1024 * 1024)
+    params = pltpu.CompilerParams(has_side_effects=True, vmem_limit_bytes=67043328)
 
     def local(x, wr, idx, w1, w3, w2):
         T, D = x.shape
@@ -488,8 +516,6 @@
         widths = [w for _, w in cols]
         L = 2 * N * C
         K = 2 * N * N
-        blocks = [(N, K, C, w) for w in widths]
-        held = [pltpu.VMEM(b, BF16) for b in blocks]
         rows, meta = _plan(x, wr, idx, C)
         xin, metas = pl.pallas_call(
             functools.partial(_dispatch, cols),
@@ -504,29 +530,24 @@
                dma((3,)), dma((3,)), dma((3,)), dma((3, N, 2)), dma((3,))],
             compiler_params=params,
         )(x, rows, meta)
-        r = pl.pallas_call(
+        out = pl.pallas_call(
             functools.partial(_experts, cols),
             name='experts',
-            out_shape=[jax.ShapeDtypeStruct(b, BF16) for b in blocks],
-            in_specs=[any_] * 4,
-            out_specs=[any_] * 3,
+            out_shape=[jax.ShapeDtypeStruct((T, D), BF16)] + [jax.ShapeDtypeStruct((N, K * C, w), BF16) for w in widths]
+            + [jax.ShapeDtypeStruct((N, len(LATER), C, w), BF16) for w in widths],
+            in_specs=[any_] * 4 + [vmem],
+            out_specs=[vmem] + [any_] * 6,
             scratch_shapes=[
                 pltpu.VMEM((D, ff), BF16), pltpu.VMEM((D, ff), BF16), pltpu.VMEM((ff, D), BF16),
-                pltpu.VMEM((2, 2, N, 2, C, D), BF16), pltpu.VMEM((2 * L, ff), BF16), pltpu.VMEM((N, N, N, 2, C, D), BF16), *held,
-                *(pltpu.VMEM((N, len(LATER), C, w), BF16) for w in widths),
-                dma((3,)), dma((2, 2)), dma((3,)), dma((3,)), dma((3,)), dma((3,)), dma((3,)), dma((3, K)), dma((3, len(LATER))), dma((3,)),
+                pltpu.VMEM((2, 2, N, 2, C, D), BF16), pltpu.VMEM((2 * L, ff), BF16), pltpu.VMEM((N, N, N, 2, C, D), BF16),
+                *(pltpu.VMEM((N, len(ONCE), C, w), BF16) for w in widths),
+                *(pltpu.VMEM((N, T, w), F32) for w in widths), *(pltpu.VMEM((2, T, w), F32) for w in widths),
+                *(pltpu.VMEM((2, T // 2, w), F32) for w in widths),
+                dma((3,)), dma((2, 2)), dma((3,)), dma((3,)), dma((3,)), dma((3,)), dma((3,)), dma((3, len(ONCE))), dma((3, len(LATER))), dma((3,)),
+                dma((N,)), dma((3, 4)), dma((3, 4)),
             ],
             compiler_params=params,
-        )(xin, w1, w3, w2)
-        return pl.pallas_call(
-            functools.partial(_combine, cols),
-            name='combine',
-            out_shape=jax.ShapeDtypeStruct((T, D), BF16),
-            in_specs=[any_] * 3 + [vmem],
-            out_specs=vmem,
-            scratch_shapes=held + [pltpu.VMEM((N, T, w), F32) for w in widths] + [pltpu.VMEM((2, T, w), F32) for w in widths]
-            + [pltpu.VMEM((2, T // 2, w), F32) for w in widths] + [pltpu.VMEM((3 * T, N * L), BF16), dma((3, N)), dma((3, 4)), dma((3, 4))],
-            compiler_params=params,
-        )(*r, metas)
+        )(xin, w1, w3, w2, metas)
+        return out[0]
 
     return jax.shard_map(local, mesh=mesh, in_specs=(tok, P(None, None), tok, wsp, wsp, wsp), out_specs=tok, check_vma=False)

time: 388 us -> 402 us (1.036)
  Pallas kernels: 377 us -> 388 us
    pallas_call x1, Pallas kernels: 175 us -> 241 us  [local(): pl.pallas_call(functools.partial(_experts, cols), name='experts', out_sha...]
    pallas_call x1 -> x0, Pallas kernels: 55.4 us -> none  [local(): pl.pallas_call(functools.partial(_combine, cols), name='combine', out_sha...]
where the time goes in v5:
time: 402 us; the launch traced here: 399 us
  Pallas kernels  388 us (97%)
  local copies, waits for them, and re-layouts  5.1 us (1%)
    pallas_call x1, Pallas kernels, local(): pl.pallas_call(functools.partial(_experts, cols), name='experts', out_sha...  241 us
    pallas_call x1, Pallas kernels, local(): pl.pallas_call(functools.partial(_dispatch, cols), name='dispatch', out_s...  147 us

profile of v5, /device:TPU:0, one launch (start us, length us, event | category | flops | bytes accessed | tf_op | source)
XLA Modules:
  0.0 399.4 jit_solution(14201910195916259286)
XLA Ops:
  0.0 0.8 copy.28
  0.8 0.4 convert_reduce_fusion
  1.2 0.2 convolution_select_fusion
  1.4 1.8 fusion.2
  3.2 0.9 select_reduce_fusion.3
  4.1 0.1 reduce_max.9
  4.2 0.1 copy.35
  4.3 0.1 copy.36
  4.5 1.3 select_reduce_fusion.2
  5.7 0.7 select_reduce_fusion
  6.4 0.1 copy.29
  6.5 0.1 sub.25
  6.6 0.1 sub.23
  6.7 0.1 sub.24
  6.8 0.1 stack.24
  6.9 0.1 stack.25
  7.0 0.1 stack_reshape.7
  7.1 0.1 copy.37
  7.2 0.1 stack_reshape_reshape.4
  7.3 0.1 reshape.84
  7.4 0.1 stack_reshape.8
  7.5 0.6 pad_maximum_fusion.meta_ref
  8.1 0.8 broadcast_in_dim.71.rows_ref
  8.9 146.9 %dispatch.1 = (bf16[4,4,4,2,32,2048]{5,4,3,2,1,0:T(8,128)(2,1)}, f32[3,4,2,16,256]{4,3,2,1,0:T(8,128)}) custom-call(bf16[256,2048]{1,0:T(8,128)(2,1)} %x_ref.1, f32[3,16,8,256]{3,2,1,0:T(8,128)} %broadcast_in_dim.71.rows_ref, f32[2,2,16,256]{3,2,1,0:T(8,128)} %pad_maximum_fusion.meta_ref), custom_call_target="tpu_custom_call" | custom-call | tf_op jit(solution)/shard_map/dispatch/pallas_call | solution.py:520
  155.8 241.2 %experts.1 = (bf16[256,2048]{1,0:T(8,128)(2,1)}, bf16[4,1024,640]{2,1,0:T(8,128)(2,1)}, bf16[4,1024,640]{2,1,0:T(8,128)(2,1)}, bf16[4,1024,768]{2,1,0:T(8,128)(2...) custom-call(bf16[4,4,4,2,32,2048]{5,4,3,2,1,0:T(8,128)(2,1)} %get-tuple-el, ...), custom_call_target="tpu_custom_call" | custom-call | tf_op jit(solution)/shard_map/experts/pallas_call | solution.py:533
  397.1 2.3 copy.43
  (10 shorter events, 0.1 us)

commit v6 on v5

--- a/solution.py
+++ b/solution.py
@@ -223,7 +223,7 @@
 
 def _spot(fo, go, cc, r):
     s = 1 - 2 * cc
-    nf = min(r, _hops(fo))
+    nf = max(r - _hops(go), 0) if cc else min(r, _hops(fo))
     ng = r - nf
     return (N + {0: 0, 1: 1, 2: s, 3: -1}[fo] * nf) % N, (N + {0: 0, 1: 1, 2: s, 3: -1}[go] * ng) % N
 
@@ -233,39 +233,14 @@
 ONCE = [k for k in WAYS if _hops(k[0]) + _hops(k[1]) > 1]
 NEAR = 2 * N * N - len(ONCE) - 1
 
-TILES = [((2, 2), (2, 1)), ((2, 3), (2, 0)), ((1, 2), (3, 2)), ((0, 2), (1, 1)),
-         ((1, 3), (1, 0)), ((3, 1), (0, 1)), ((3, 3), (3, 0)), ((0, 3), (0, 0))]
-LAG = 2
-
-
-def _messages():
-    seen, steps = set(), []
-    for tile in TILES:
-        out = []
-        for zo, yo in tile:
-            seen.add((zo, yo))
-            for cc in range(2):
-                out.append((2, yo, zo, cc))
-        for o in dict.fromkeys(v[0] for v in tile):
-            if all((o, k) in seen for k in range(N)) and not any(m[0] == 1 and m[1] == o for t in steps for m in t):
-                out += [(1, o, do, cc) for do in (2, 1, 3, 0) for cc in range(2)]
-        for o in dict.fromkeys(v[1] for v in tile):
-            if all((k, o) in seen for k in range(N)) and not any(m[0] == 0 and m[2] == o for t in steps for m in t):
-                out += [(0, do, o, cc) for do in (2, 1, 3, 0) for cc in range(2)]
-        steps.append(out)
-    assert sum(len(t) for t in steps) == 3 * len(WAYS)
-    return steps
-
-
-def _schedule():
-    first = _messages()
-    left = {}
-    for st, out in enumerate(first):
-        for m in out:
-            n = _hops(m[1]) + _hops(m[2])
-            for r in range(1, n):
-                left.setdefault(min(st + LAG * r, len(TILES)), []).append((r, (m[0], m[1:], r)))
-    return first, [[v for _, v in sorted(left.get(st, []), key=lambda t: t[0])] for st in range(len(TILES) + 1)]
+TILES = [((2, 1), (2, 3)), ((1, 2), (3, 2)), ((2, 2), (2, 0)), ((1, 1), (3, 3)),
+         ((1, 3), (3, 1)), ((0, 2), (0, 0)), ((1, 0), (3, 0)), ((0, 1), (0, 3))]
+
+
+def _later(parts, r, hops):
+    keys = [k for k in ONCE if _hops(k[0]) + _hops(k[1]) in hops and _hops(k[0]) + _hops(k[1]) > r]
+    keys = sorted(keys, key=lambda k: -_hops(k[0]) - _hops(k[1]))
+    return [(p, k, r) for k in keys for p in parts]
 
 
 def _pick(values, s):
@@ -284,7 +259,6 @@
     steps = len(TILES)
     base = ((y, x), (z, x), (z, y))
     axis = (z, y, x)
-    first, later = _schedule()
     loads = [pltpu.make_async_copy(s.at[0], d, wsem.at[q]) for q, (s, d) in enumerate(((w1_ref, w1), (w3_ref, w3), (w2_ref, w2)))]
 
     def cell(st, q):
@@ -308,18 +282,35 @@
     def slot(p, b, d):
         return R[p].at[:, pl.ds(((b * N + d) * 2 + c) * C, C)]
 
-    def put(p, fo, go, cc):
+    def put(p, fo, go, cc, lead, src):
         bo, do = _bd(p, fo, go)
         b, d, c2 = (base[p][0] + bo) % N, (base[p][1] + do) % N, (c + cc) % 2
-        src = (ob.at[:, b, d, c2, :, cs[0]], ob.at[b, :, d, c2, :, cs[1]], ob.at[b, d, :, c2, :, cs[2]])[p]
+        dst = R[p].at[lead, pl.ds(((base[p][0] * N + base[p][1]) * 2 + c) * C, C)]
         n = _hops(fo) + _hops(go)
         if n > 1:
             k = ONCE.index((fo, go, cc))
-            _copy(src, rl[p].at[:, k], lsend.at[p], rrecv.at[p, k], at(p, *_spot(fo, go, cc, 1), 0)).start()
+            _copy(src, rl[p].at[lead, k], lsend.at[p], rrecv.at[p, k], at(p, *_spot(fo, go, cc, 1), 0)).start()
         elif n + cc:
-            _copy(src, slot(p, *base[p]), send.at[p], recv.at[p], _plane(p, me, b, d, c2)).start()
+            _copy(src, dst, send.at[p], recv.at[p], _plane(p, me, b, d, c2)).start()
         else:
-            pltpu.make_async_copy(src, slot(p, *base[p]), own.at[p]).start()
+            pltpu.make_async_copy(src, dst, own.at[p]).start()
+
+    def give(st):
+        for cc in range(2):
+            c2 = (c + cc) % 2
+            for q in range(2):
+                zo, yo = TILES[st][q]
+                zt, yv = cell(st, q)
+                put(2, yo, zo, cc, slice(None), ob.at[zt, yv, :, c2, :, cs[2]])
+        for do in (2, 1, 3, 0):
+            x2 = (x + do) % N
+            for cc in range(2):
+                c2 = (c + cc) % 2
+                for q in range(2):
+                    zo, yo = TILES[st][q]
+                    zt, yv = cell(st, q)
+                    put(0, do, yo, cc, zt, ob.at[zt, yv, x2, c2, :, cs[0]])
+                    put(1, zo, do, cc, yv, ob.at[zt, yv, x2, c2, :, cs[1]])
 
     def forward(p, key, r):
         fo, go, cc = key
@@ -376,10 +367,7 @@
         for st in range(steps):
             @pl.when(s == st)
             def _():
-                for m in first[st]:
-                    put(*m)
-                for v in later[st]:
-                    forward(*v)
+                give(st)
 
     S, Q, H = (s0, s1, s2), (q0, q1, q2), (h0, h1, h2)
     T = y_ref.shape[0]
@@ -430,21 +418,21 @@
             S[p][sides[q], halves[q]] += H[p][q]
             _copy(S[p].at[sides[q]], Q[p].at[q], ssend.at[p, 2 + q], srecv.at[p, 2 + q], side(p, q)).start()
 
-    rest = later[steps]
-    for v in rest:
-        if v[0] == 2 or v[2] == 1:
+    def onwards(*args):
+        for v in _later(*args):
             forward(*v)
-    more = [v for v in rest if not (v[0] == 2 or v[2] == 1)]
+
+    onwards((2,), 1, (2, 3, 4))
+    onwards((1, 0), 1, (3, 4))
+    onwards((2,), 2, (3, 4))
+    onwards((1, 0), 1, (2,))
+    onwards((2,), 3, (4,))
+    onwards((1, 0), 2, (3, 4))
     gather(2)
     partial(2, 2)
     halfway(2)
-    for v in more:
-        if v[2] == 2:
-            forward(*v)
+    onwards((1, 0), 3, (4,))
     partial(2, 1)
-    for v in more:
-        if v[2] == 3:
-            forward(*v)
     partial(2, 3)
     onward(2)
     partial(2, 0)

time: 402 us -> 366 us (0.910)
  Pallas kernels: 388 us -> 355 us
    pallas_call x1, Pallas kernels: 241 us -> 208 us  [local(): pl.pallas_call(functools.partial(_experts, cols), name='experts', out_sha...]
where the time goes in v6:
time: 366 us
  Pallas kernels  355 us (97%)
  local copies, waits for them, and re-layouts  5.1 us (1%)
  other arithmetic  4 us (1%)
    pallas_call x1, Pallas kernels, local(): pl.pallas_call(functools.partial(_experts, cols), name='experts', out_sha...  208 us
    pallas_call x1, Pallas kernels, local(): pl.pallas_call(functools.partial(_dispatch, cols), name='dispatch', out_s...  147 us

profile of v6, /device:TPU:0, one launch (start us, length us, event | category | flops | bytes accessed | tf_op | source)
XLA Modules:
  0.0 365.8 jit_solution(4860351915071974756)
XLA Ops:
  0.0 0.8 copy.28
  0.8 0.4 convert_reduce_fusion
  1.2 0.2 convolution_select_fusion
  1.4 1.8 fusion.2
  3.2 0.9 select_reduce_fusion.3
  4.1 0.1 reduce_max.9
  4.2 0.1 copy.35
  4.3 0.1 copy.36
  4.5 1.3 select_reduce_fusion.2
  5.7 0.7 select_reduce_fusion
  6.4 0.1 copy.29
  6.5 0.1 sub.25
  6.6 0.1 sub.23
  6.7 0.1 sub.24
  6.8 0.1 stack.24
  6.9 0.1 stack.25
  7.0 0.1 stack_reshape.7
  7.1 0.1 copy.37
  7.2 0.1 stack_reshape_reshape.4
  7.3 0.1 reshape.84
  7.4 0.1 stack_reshape.8
  7.5 0.6 pad_maximum_fusion.meta_ref
  8.1 0.8 broadcast_in_dim.71.rows_ref
  8.9 146.9 %dispatch.1 = (bf16[4,4,4,2,32,2048]{5,4,3,2,1,0:T(8,128)(2,1)}, f32[3,4,2,16,256]{4,3,2,1,0:T(8,128)}) custom-call(bf16[256,2048]{1,0:T(8,128)(2,1)} %x_ref.1, f32[3,16,8,256]{3,2,1,0:T(8,128)} %broadcast_in_dim.71.rows_ref, f32[2,2,16,256]{3,2,1,0:T(8,128)} %pad_maximum_fusion.meta_ref), custom_call_target="tpu_custom_call" | custom-call | tf_op jit(solution)/shard_map/dispatch/pallas_call | solution.py:508
  155.8 207.6 %experts.1 = (bf16[256,2048]{1,0:T(8,128)(2,1)}, bf16[4,1024,640]{2,1,0:T(8,128)(2,1)}, bf16[4,1024,640]{2,1,0:T(8,128)(2,1)}, bf16[4,1024,768]{2,1,0:T(8,128)(2...) custom-call(bf16[4,4,4,2,32,2048]{5,4,3,2,1,0:T(8,128)(2,1)} %get-tuple-el, ...), custom_call_target="tpu_custom_call" | custom-call | tf_op jit(solution)/shard_map/experts/pallas_call | solution.py:521
  363.5 2.3 copy.43
  (10 shorter events, 0.1 us)

commit v7 on v6

--- a/solution.py
+++ b/solution.py
@@ -176,18 +176,21 @@
 
     for p in parts:
         select(p, 0)
+    for p in parts:
         for k in sides:
             pass_b(p, k)
     for p in parts:
+        relay(p, 0)
         pass_b(p, 2)
+    for p in parts:
         for bo in sides:
             select(p, bo)
-        relay(p, 0)
     for p in parts:
         for k in range(N):
             for q in range(2):
                 _wait(ag[p].at[0, 0, halves[q]], brecv.at[p, 2 + q, k])
         select(p, 2)
+    for p in parts:
         for bo in sides:
             relay(p, bo)
     for p in parts:
@@ -222,10 +225,10 @@
 
 
 def _spot(fo, go, cc, r):
-    s = 1 - 2 * cc
+    sf, sg = (1 - 2 * ((o + cc) % 2) for o in (go, fo))
     nf = max(r - _hops(go), 0) if cc else min(r, _hops(fo))
     ng = r - nf
-    return (N + {0: 0, 1: 1, 2: s, 3: -1}[fo] * nf) % N, (N + {0: 0, 1: 1, 2: s, 3: -1}[go] * ng) % N
+    return (N + {0: 0, 1: 1, 2: sf, 3: -1}[fo] * nf) % N, (N + {0: 0, 1: 1, 2: sg, 3: -1}[go] * ng) % N
 
 
 WAYS = [(fo, go, cc) for fo in (2, 1, 3, 0) for go in (2, 1, 3, 0) for cc in range(2)]
@@ -237,10 +240,13 @@
          ((1, 3), (3, 1)), ((0, 2), (0, 0)), ((1, 0), (3, 0)), ((0, 1), (0, 3))]
 
 
-def _later(parts, r, hops):
-    keys = [k for k in ONCE if _hops(k[0]) + _hops(k[1]) in hops and _hops(k[0]) + _hops(k[1]) > r]
-    keys = sorted(keys, key=lambda k: -_hops(k[0]) - _hops(k[1]))
-    return [(p, k, r) for k in keys for p in parts]
+def _ready(p, fo, go):
+    return max(st for st, t in enumerate(TILES) for zo, yo in t if ((yo == go), (zo == fo), (zo, yo) == (go, fo))[p])
+
+
+def _later(parts, r):
+    n = {k: _hops(k[0]) + _hops(k[1]) for k in ONCE}
+    return sorted(((p, k, r) for k in ONCE for p in parts if n[k] > r), key=lambda v: (_ready(v[0], *v[1][:2]), -n[v[1]], -v[0]))
 
 
 def _pick(values, s):
@@ -346,7 +352,7 @@
 
         @pl.when(s == 0)
         def _():
-            for q in loads:
+            for q in loads[:2]:
                 q.wait()
 
         @pl.loop(0, ff // fs)
@@ -356,6 +362,10 @@
             a = jnp.dot(xt, w1[:, fc], preferred_element_type=F32)
             b = jnp.dot(xt, w3[:, fc], preferred_element_type=F32)
             hb[:, fc] = (jax.nn.silu(a) * b).astype(BF16)
+
+        @pl.when(s == 0)
+        def _():
+            loads[2].wait()
 
         @pl.loop(0, D // ds)
         def _(f):
@@ -412,48 +422,42 @@
         for q in range(2):
             _copy(S[p].at[2, halves[q]], H[p].at[q], ssend.at[p, q], srecv.at[p, q], side(p, q)).start()
 
-    def onward(p):
-        for q in range(2):
-            _wait(H[p].at[q], srecv.at[p, q])
-            S[p][sides[q], halves[q]] += H[p][q]
-            _copy(S[p].at[sides[q]], Q[p].at[q], ssend.at[p, 2 + q], srecv.at[p, 2 + q], side(p, q)).start()
+    def hand(p, q, e, at_):
+        _copy(S[p].at[sides[q], halves[e]], Q[p].at[q, halves[e]], ssend.at[p, at_ + q], srecv.at[p, at_ + q], side(p, q)).start()
 
     def onwards(*args):
         for v in _later(*args):
             forward(*v)
 
-    onwards((2,), 1, (2, 3, 4))
-    onwards((1, 0), 1, (3, 4))
-    onwards((2,), 2, (3, 4))
-    onwards((1, 0), 1, (2,))
-    onwards((2,), 3, (4,))
-    onwards((1, 0), 2, (3, 4))
-    gather(2)
-    partial(2, 2)
-    halfway(2)
-    onwards((1, 0), 3, (4,))
-    partial(2, 1)
-    partial(2, 3)
-    onward(2)
-    partial(2, 0)
-    for p in (1, 0):
+    onwards((2, 1, 0), 1)
+    onwards((2,), 2)
+    onwards((2,), 3)
+    onwards((1, 0), 2)
+    for p in (2, 1, 0):
         gather(p)
         partial(p, 2)
         halfway(p)
-        partial(p, 1)
-        partial(p, 3)
-        onward(p)
+        if p == 2:
+            onwards((1, 0), 3)
+        for q in range(2):
+            partial(p, sides[q])
+            hand(p, q, 1 - q, 2)
+        for q in range(2):
+            _wait(H[p].at[q], srecv.at[p, q])
+            S[p][sides[q], halves[q]] += H[p][q]
+            hand(p, q, q, 4)
         partial(p, 0)
     for p in (2, 1, 0):
         t = S[p][0]
         for q in range(2):
-            _wait(Q[p].at[q], srecv.at[p, 2 + q])
+            for e in (2, 4):
+                _wait(H[p].at[q], srecv.at[p, e + q])
             t += Q[p][q]
         y_ref[:, cs[p]] = t.astype(BF16)
     for p in range(3):
         for q in range(2):
-            _wait(H[p].at[q], ssend.at[p, q])
-            _wait(Q[p].at[q], ssend.at[p, 2 + q])
+            for e in (0, 2, 4):
+                _wait(H[p].at[q], ssend.at[p, e + q])
         _wait(R[p].at[:, pl.ds(0, NEAR * C)], send.at[p])
         _wait(R[p].at[:, pl.ds(0, len(ONCE) * C)], lsend.at[p])
         _wait(R[p].at[:, pl.ds(0, len(ONCE) * C)], fsend.at[p])
@@ -532,7 +536,7 @@
                 *(pltpu.VMEM((N, T, w), F32) for w in widths), *(pltpu.VMEM((2, T, w), F32) for w in widths),
                 *(pltpu.VMEM((2, T // 2, w), F32) for w in widths),
                 dma((3,)), dma((2, 2)), dma((3,)), dma((3,)), dma((3,)), dma((3,)), dma((3,)), dma((3, len(ONCE))), dma((3, len(LATER))), dma((3,)),
-                dma((N,)), dma((3, 4)), dma((3, 4)),
+                dma((N,)), dma((3, 6)), dma((3, 6)),
             ],
             compiler_params=params,
         )(xin, w1, w3, w2, metas)

time: 366 us -> 358 us (0.978)
  Pallas kernels: 355 us -> 346 us
    pallas_call x1, Pallas kernels: 147 us -> 140 us  [local(): pl.pallas_call(functools.partial(_dispatch, cols), name='dispatch', out_s...]
where the time goes in v7:
time: 358 us
  Pallas kernels  346 us (97%)
  local copies, waits for them, and re-layouts  5.1 us (1%)
  other arithmetic  4 us (1%)
    pallas_call x1, Pallas kernels, local(): pl.pallas_call(functools.partial(_experts, cols), name='experts', out_sha...  206 us
    pallas_call x1, Pallas kernels, local(): pl.pallas_call(functools.partial(_dispatch, cols), name='dispatch', out_s...  140 us

profile of v7, /device:TPU:0, one launch (start us, length us, event | category | flops | bytes accessed | tf_op | source)
XLA Modules:
  0.0 357.7 jit_solution(8101698768200109990)
XLA Ops:
  0.0 0.8 copy.28
  0.8 0.4 convert_reduce_fusion
  1.2 0.2 convolution_select_fusion
  1.4 1.8 fusion.2
  3.2 0.9 select_reduce_fusion.3
  4.1 0.1 reduce_max.9
  4.2 0.1 copy.35
  4.3 0.1 copy.36
  4.5 1.3 select_reduce_fusion.2
  5.7 0.7 select_reduce_fusion
  6.4 0.1 copy.29
  6.5 0.1 sub.25
  6.6 0.1 sub.23
  6.7 0.1 sub.24
  6.8 0.1 stack.24
  6.9 0.1 stack.25
  7.0 0.1 stack_reshape.7
  7.1 0.1 copy.37
  7.2 0.1 stack_reshape_reshape.4
  7.3 0.1 reshape.84
  7.4 0.1 stack_reshape.8
  7.5 0.6 pad_maximum_fusion.meta_ref
  8.1 0.8 broadcast_in_dim.71.rows_ref
  8.9 140.3 %dispatch.1 = (bf16[4,4,4,2,32,2048]{5,4,3,2,1,0:T(8,128)(2,1)}, f32[3,4,2,16,256]{4,3,2,1,0:T(8,128)}) custom-call(bf16[256,2048]{1,0:T(8,128)(2,1)} %x_ref.1, f32[3,16,8,256]{3,2,1,0:T(8,128)} %broadcast_in_dim.71.rows_ref, f32[2,2,16,256]{3,2,1,0:T(8,128)} %pad_maximum_fusion.meta_ref), custom_call_target="tpu_custom_call" | custom-call | tf_op jit(solution)/shard_map/dispatch/pallas_call | solution.py:512
  149.3 206.1 %experts.1 = (bf16[256,2048]{1,0:T(8,128)(2,1)}, bf16[4,1024,640]{2,1,0:T(8,128)(2,1)}, bf16[4,1024,640]{2,1,0:T(8,128)(2,1)}, bf16[4,1024,768]{2,1,0:T(8,128)(2...) custom-call(bf16[4,4,4,2,32,2048]{5,4,3,2,1,0:T(8,128)(2,1)} %get-tuple-el, ...), custom_call_target="tpu_custom_call" | custom-call | tf_op jit(solution)/shard_map/experts/pallas_call | solution.py:525
  355.4 2.3 copy.43
  (10 shorter events, 0.1 us)

commit v8 on v7

--- a/solution.py
+++ b/solution.py
@@ -236,17 +236,24 @@
 ONCE = [k for k in WAYS if _hops(k[0]) + _hops(k[1]) > 1]
 NEAR = 2 * N * N - len(ONCE) - 1
 
-TILES = [((2, 1), (2, 3)), ((1, 2), (3, 2)), ((2, 2), (2, 0)), ((1, 1), (3, 3)),
-         ((1, 3), (3, 1)), ((0, 2), (0, 0)), ((1, 0), (3, 0)), ((0, 1), (0, 3))]
+TILES = [((2, 2), (0, 2)), ((1, 2), (3, 2)), ((2, 1), (2, 3)), ((2, 0), (0, 0)),
+         ((1, 1), (3, 3)), ((1, 3), (3, 1)), ((1, 0), (3, 0)), ((0, 1), (0, 3))]
+LAG = 3
 
 
 def _ready(p, fo, go):
     return max(st for st, t in enumerate(TILES) for zo, yo in t if ((yo == go), (zo == fo), (zo, yo) == (go, fo))[p])
 
 
-def _later(parts, r):
+def _when(p, key, r):
+    n, st = _hops(key[0]) + _hops(key[1]), _ready(p, *key[:2]) + LAG * r
+    return st if n > 2 and st < len(TILES) else len(TILES)
+
+
+def _later(parts, r, at=len(TILES)):
     n = {k: _hops(k[0]) + _hops(k[1]) for k in ONCE}
-    return sorted(((p, k, r) for k in ONCE for p in parts if n[k] > r), key=lambda v: (_ready(v[0], *v[1][:2]), -n[v[1]], -v[0]))
+    return sorted(((p, k, r) for k in ONCE for p in parts if n[k] > r and _when(p, k, r) == at),
+                  key=lambda v: (_ready(v[0], *v[1][:2]), -n[v[1]], -v[0]))
 
 
 def _pick(values, s):
@@ -378,6 +385,9 @@
             @pl.when(s == st)
             def _():
                 give(st)
+                for r in (1, 2, 3):
+                    for v in _later((2, 1, 0), r, st):
+                        forward(*v)
 
     S, Q, H = (s0, s1, s2), (q0, q1, q2), (h0, h1, h2)
     T = y_ref.shape[0]

time: 358 us -> 360 us (level)
  no operation moved by 1% of the time
where the time goes in v8:
time: 360 us; the launch traced here: 359 us
  Pallas kernels  348 us (97%)
  local copies, waits for them, and re-layouts  5.1 us (1%)
  other arithmetic  4 us (1%)
    pallas_call x1, Pallas kernels, local(): pl.pallas_call(functools.partial(_experts, cols), name='experts', out_sha...  207 us
    pallas_call x1, Pallas kernels, local(): pl.pallas_call(functools.partial(_dispatch, cols), name='dispatch', out_s...  140 us

profile of v8, /device:TPU:0, one launch (start us, length us, event | category | flops | bytes accessed | tf_op | source)
XLA Modules:
  0.0 359.0 jit_solution(4244472010852932931)
XLA Ops:
  0.0 0.8 copy.28
  0.8 0.4 convert_reduce_fusion
  1.2 0.2 convolution_select_fusion
  1.4 1.8 fusion.2
  3.2 0.9 select_reduce_fusion.3
  4.1 0.1 reduce_max.9
  4.2 0.1 copy.35
  4.3 0.1 copy.36
  4.5 1.3 select_reduce_fusion.2
  5.7 0.7 select_reduce_fusion
  6.4 0.1 copy.29
  6.5 0.1 sub.25
  6.6 0.1 sub.23
  6.7 0.1 sub.24
  6.8 0.1 stack.24
  6.9 0.1 stack.25
  7.0 0.1 stack_reshape.7
  7.1 0.1 copy.37
  7.2 0.1 stack_reshape_reshape.4
  7.3 0.1 reshape.84
  7.4 0.1 stack_reshape.8
  7.5 0.6 pad_maximum_fusion.meta_ref
  8.1 0.8 broadcast_in_dim.71.rows_ref
  8.9 140.3 %dispatch.1 = (bf16[4,4,4,2,32,2048]{5,4,3,2,1,0:T(8,128)(2,1)}, f32[3,4,2,16,256]{4,3,2,1,0:T(8,128)}) custom-call(bf16[256,2048]{1,0:T(8,128)(2,1)} %x_ref.1, f32[3,16,8,256]{3,2,1,0:T(8,128)} %broadcast_in_dim.71.rows_ref, f32[2,2,16,256]{3,2,1,0:T(8,128)} %pad_maximum_fusion.meta_ref), custom_call_target="tpu_custom_call" | custom-call | tf_op jit(solution)/shard_map/dispatch/pallas_call | solution.py:522
  149.3 207.5 %experts.1 = (bf16[256,2048]{1,0:T(8,128)(2,1)}, bf16[4,1024,640]{2,1,0:T(8,128)(2,1)}, bf16[4,1024,640]{2,1,0:T(8,128)(2,1)}, bf16[4,1024,768]{2,1,0:T(8,128)(2...) custom-call(bf16[4,4,4,2,32,2048]{5,4,3,2,1,0:T(8,128)(2,1)} %get-tuple-el, ...), custom_call_target="tpu_custom_call" | custom-call | tf_op jit(solution)/shard_map/experts/pallas_call | solution.py:535
  356.7 2.3 copy.43
  (10 shorter events, 0.1 us)

commit v9 on v7

--- a/solution.py
+++ b/solution.py
@@ -11,6 +11,8 @@
 F32 = jnp.float32
 BF16 = jnp.bfloat16
 N = 4
+PAIR, PARTS = range(2), range(3)
+FAR_FIRST = (2, 1, 3, 0)
 
 
 def _cols(d):
@@ -70,7 +72,7 @@
     axis = (z, y, x)
     base = ((z, y, x), (y, x, z), (x, z, y))
     which = (0, 0, 1)
-    parts = range(3)
+    parts = PARTS
     sides = (1, 3)
     halves = (pl.ds(0, h), pl.ds(h, h))
 
@@ -84,12 +86,12 @@
 
     def give_b(p, k, src):
         a, b, d = base[p]
-        for q in range(2):
+        for q in PAIR:
             _copy(src, ag[p].at[(a + k) % N, b], bsend.at[p, q, k], brecv.at[p, q, k], to_b(p, sides[q])).start()
 
     def pass_b(p, k):
         a, b, d = base[p]
-        for q in range(2):
+        for q in PAIR:
             _wait(ag[p].at[0, 0], brecv.at[p, q, k])
             blk = ag[p].at[(a + k) % N, (b + (3, 1)[q]) % N, halves[q]]
             _copy(blk, blk, bsend.at[p, 2 + q, k], brecv.at[p, 2 + q, k], to_b(p, sides[q])).start()
@@ -97,7 +99,7 @@
     for p in parts:
         a, b, d = base[p]
         blk = x_ref.at[:, pl.ds(*cols[p])]
-        for q in range(2):
+        for q in PAIR:
             _copy(blk, ag[p].at[a, b], asend.at[p, q], arecv.at[p, q], to_a(p, sides[q])).start()
         pltpu.make_async_copy(blk, ag[p].at[a, b], lown.at[p, 0]).start()
     for p in parts:
@@ -114,7 +116,7 @@
         give_b(p, 0, x_ref.at[:, pl.ds(*cols[p])])
     for p in parts:
         a, b, d = base[p]
-        for q in range(2):
+        for q in PAIR:
             _wait(ag[p].at[0, 0], arecv.at[p, q])
             blk = ag[p].at[(a + (3, 1)[q]) % N, b, halves[q]]
             _copy(blk, blk, asend.at[p, 2 + q], arecv.at[p, 2 + q], to_a(p, sides[q])).start()
@@ -130,7 +132,7 @@
         pass_b(p, 0)
     for p in parts:
         a, b, d = base[p]
-        for q in range(2):
+        for q in PAIR:
             _wait(ag[p].at[0, 0, halves[q]], arecv.at[p, 2 + q])
         give_b(p, 2, ag[p].at[(a + 2) % N, b])
         _wait(ag[p].at[0, 0], lown.at[p, 0])
@@ -153,8 +155,8 @@
             r = lax.dot_general(hot, ag[p][a, bs], (((0,), (0,)), ((), ())), preferred_element_type=F32)
             sb[p][a, bo] = r.astype(BF16).reshape(2 * N, C, w)
 
-        for do in (2, 1, 3, 0):
-            for cc in range(2):
+        for do in FAR_FIRST:
+            for cc in PAIR:
                 s = 1 - 2 * cc
                 src = sb[p].at[:, bo, (d + do) % N * 2 + (c + cc) % 2]
                 if do == 2:
@@ -168,7 +170,7 @@
 
     def relay(p, bo):
         a, b, d = base[p]
-        for cc in range(2):
+        for cc in PAIR:
             s = 1 - 2 * cc
             _wait(rl[p].at[bo, cc], rrecv.at[p, bo, cc])
             to = _dev(*_order(p, a, b, (d + N + s) % N), (c + cc) % 2)
@@ -187,7 +189,7 @@
             select(p, bo)
     for p in parts:
         for k in range(N):
-            for q in range(2):
+            for q in PAIR:
                 _wait(ag[p].at[0, 0, halves[q]], brecv.at[p, 2 + q, k])
         select(p, 2)
     for p in parts:
@@ -204,7 +206,7 @@
         for k in (1, 2, 3):
             _wait(mb.at[p, 0], msend.at[p, k])
         _wait(rows_ref.at[p, pl.ds(0, N * N - 1)], tsend.at[p])
-        for q in range(2):
+        for q in PAIR:
             _wait(ag[p].at[0, 0], asend.at[p, q])
             _wait(ag[p].at[0, 0, halves[q]], asend.at[p, 2 + q])
             for k in range(N):
@@ -231,7 +233,7 @@
     return (N + {0: 0, 1: 1, 2: sf, 3: -1}[fo] * nf) % N, (N + {0: 0, 1: 1, 2: sg, 3: -1}[go] * ng) % N
 
 
-WAYS = [(fo, go, cc) for fo in (2, 1, 3, 0) for go in (2, 1, 3, 0) for cc in range(2)]
+WAYS = [(fo, go, cc) for fo in FAR_FIRST for go in FAR_FIRST for cc in PAIR]
 LATER = [(k, r) for r in (2, 3) for k in WAYS if _hops(k[0]) + _hops(k[1]) > r]
 ONCE = [k for k in WAYS if _hops(k[0]) + _hops(k[1]) > 1]
 NEAR = 2 * N * N - len(ONCE) - 1
@@ -272,7 +274,7 @@
         return (z + zo) % N, (y + yo) % N
 
     def load(st):
-        for q in range(2):
+        for q in PAIR:
             zt, yv = cell(st, q)
             pltpu.make_async_copy(xin.at[zt, yv], xb.at[st % 2, q], xsem.at[st % 2, q]).start()
 
@@ -302,17 +304,17 @@
             pltpu.make_async_copy(src, dst, own.at[p]).start()
 
     def give(st):
-        for cc in range(2):
+        for cc in PAIR:
             c2 = (c + cc) % 2
-            for q in range(2):
+            for q in PAIR:
                 zo, yo = TILES[st][q]
                 zt, yv = cell(st, q)
                 put(2, yo, zo, cc, slice(None), ob.at[zt, yv, :, c2, :, cs[2]])
-        for do in (2, 1, 3, 0):
+        for do in FAR_FIRST:
             x2 = (x + do) % N
-            for cc in range(2):
+            for cc in PAIR:
                 c2 = (c + cc) % 2
-                for q in range(2):
+                for q in PAIR:
                     zo, yo = TILES[st][q]
                     zt, yv = cell(st, q)
                     put(0, do, yo, cc, zt, ob.at[zt, yv, x2, c2, :, cs[0]])
@@ -328,7 +330,7 @@
             k = LATER.index((key, r))
             buf, sem = rm[p].at[:, k], irecv.at[p, k]
         _wait(buf, sem)
-        hop = [(there[q] + N - here[q]) % N for q in range(2)]
+        hop = [(there[q] + N - here[q]) % N for q in PAIR]
         if r + 1 == _hops(fo) + _hops(go):
             bs, ds = ((base[p][q] + N - v) % N for q, v in enumerate(_bd(p, *here)))
             _copy(buf, slot(p, bs, ds), fsend.at[p], recv.at[p], at(p, *hop, cc)).start()
@@ -340,14 +342,14 @@
 
     @pl.loop(0, steps)
     def _(s):
-        zt = [(z + _pick([t[q][0] for t in TILES], s)) % N for q in range(2)]
-        yt = [(y + _pick([t[q][1] for t in TILES], s)) % N for q in range(2)]
+        zt = [(z + _pick([t[q][0] for t in TILES], s)) % N for q in PAIR]
+        yt = [(y + _pick([t[q][1] for t in TILES], s)) % N for q in PAIR]
         for st in range(steps - 1):
             @pl.when(s == st)
             def _():
                 load(st + 1)
 
-        for q in range(2):
+        for q in PAIR:
             _wait(xb.at[0, q], xsem.at[s % 2, q])
 
         @pl.when(s == 0)
@@ -389,10 +391,12 @@
     def room(k, p):
         return (w1, w3)[k // 2].at[pl.ds(k % 2 * N * L, N * L), pl.ds(0, cols[p][1])]
 
-    def gather(p):
+    def arrived(p):
         _wait(slot(p, 0, 0), own.at[p])
         _wait(R[p].at[:, pl.ds(0, (2 * N * N - 1) * C)], recv.at[p])
-        for k in (2, 1, 3, 0):
+
+    def fetch(p, *ks):
+        for k in ks:
             pltpu.make_async_copy(R[p].at[(axis[p] + k) % N], room(k, p), bsem.at[k]).start()
 
     def partial(p, k):
@@ -407,7 +411,7 @@
             hot = lax.broadcasted_iota(jnp.int32, (T, L), 0).astype(F32) == tab
             m = jnp.where(hot, g, 0.0)
             here = pl.ds(pl.multiple_of(b * L, L), L)
-            for q in range(3):
+            for q in PARTS:
                 part = m.astype(BF16)
                 w2[q * T:(q + 1) * T, here] = part
                 m = m - part.astype(F32)
@@ -419,7 +423,7 @@
         return _along(p, me, (axis[p] + sides[q]) % N)
 
     def halfway(p):
-        for q in range(2):
+        for q in PAIR:
             _copy(S[p].at[2, halves[q]], H[p].at[q], ssend.at[p, q], srecv.at[p, q], side(p, q)).start()
 
     def hand(p, q, e, at_):
@@ -433,29 +437,49 @@
     onwards((2,), 2)
     onwards((2,), 3)
     onwards((1, 0), 2)
-    for p in (2, 1, 0):
-        gather(p)
-        partial(p, 2)
-        halfway(p)
-        if p == 2:
-            onwards((1, 0), 3)
-        for q in range(2):
+    def outward(p):
+        for q in PAIR:
             partial(p, sides[q])
             hand(p, q, 1 - q, 2)
-        for q in range(2):
+
+    def finish(p):
+        for q in PAIR:
             _wait(H[p].at[q], srecv.at[p, q])
             S[p][sides[q], halves[q]] += H[p][q]
             hand(p, q, q, 4)
-        partial(p, 0)
+
+    arrived(2)
+    fetch(2, *FAR_FIRST)
+    partial(2, 2)
+    halfway(2)
+    onwards((1, 0), 3)
+    outward(2)
+    partial(2, 0)
+    finish(2)
+    arrived(1)
+    fetch(1, *FAR_FIRST)
+    partial(1, 2)
+    halfway(1)
+    outward(1)
+    arrived(0)
+    fetch(0, 2, 1, 3)
+    partial(0, 2)
+    halfway(0)
+    outward(0)
+    finish(1)
+    partial(1, 0)
+    fetch(0, 0)
+    finish(0)
+    partial(0, 0)
     for p in (2, 1, 0):
         t = S[p][0]
-        for q in range(2):
+        for q in PAIR:
             for e in (2, 4):
                 _wait(H[p].at[q], srecv.at[p, e + q])
             t += Q[p][q]
         y_ref[:, cs[p]] = t.astype(BF16)
-    for p in range(3):
-        for q in range(2):
+    for p in PARTS:
+        for q in PAIR:
             for e in (0, 2, 4):
                 _wait(H[p].at[q], ssend.at[p, e + q])
         _wait(R[p].at[:, pl.ds(0, NEAR * C)], send.at[p])

time: 358 us -> 353 us (0.986)
  Pallas kernels: 346 us -> 341 us
    pallas_call x1, Pallas kernels: 206 us -> 201 us  [local(): pl.pallas_call(functools.partial(_experts, cols), name='experts', out_sha...]
where the time goes in v9:
time: 353 us; the launch traced here: 352 us
  Pallas kernels  341 us (97%)
  local copies, waits for them, and re-layouts  5.1 us (1%)
  other arithmetic  4 us (1%)
    pallas_call x1, Pallas kernels, local(): pl.pallas_call(functools.partial(_experts, cols), name='experts', out_sha...  201 us
    pallas_call x1, Pallas kernels, local(): pl.pallas_call(functools.partial(_dispatch, cols), name='dispatch', out_s...  140 us

profile of v9, /device:TPU:0, one launch (start us, length us, event | category | flops | bytes accessed | tf_op | source)
XLA Modules:
  0.0 352.5 jit_solution(17266332599020577110)
XLA Ops:
  0.0 0.8 copy.28
  0.8 0.4 convert_reduce_fusion
  1.2 0.2 convolution_select_fusion
  1.4 1.8 fusion.2
  3.2 0.9 select_reduce_fusion.3
  4.1 0.1 reduce_max.9
  4.2 0.1 copy.35
  4.3 0.1 copy.36
  4.5 1.3 select_reduce_fusion.2
  5.7 0.7 select_reduce_fusion
  6.4 0.1 copy.29
  6.5 0.1 sub.25
  6.6 0.1 sub.23
  6.7 0.1 sub.24
  6.8 0.1 stack.24
  6.9 0.1 stack.25
  7.0 0.1 stack_reshape.7
  7.1 0.1 copy.37
  7.2 0.1 stack_reshape_reshape.4
  7.3 0.1 reshape.84
  7.4 0.1 stack_reshape.8
  7.5 0.6 pad_maximum_fusion.meta_ref
  8.1 0.8 broadcast_in_dim.71.rows_ref
  8.9 140.3 %dispatch.1 = (bf16[4,4,4,2,32,2048]{5,4,3,2,1,0:T(8,128)(2,1)}, f32[3,4,2,16,256]{4,3,2,1,0:T(8,128)}) custom-call(bf16[256,2048]{1,0:T(8,128)(2,1)} %x_ref.1, f32[3,16,8,256]{3,2,1,0:T(8,128)} %broadcast_in_dim.71.rows_ref, f32[2,2,16,256]{3,2,1,0:T(8,128)} %pad_maximum_fusion.meta_ref), custom_call_target="tpu_custom_call" | custom-call | tf_op jit(solution)/shard_map/dispatch/pallas_call | solution.py:536
  149.3 200.9 %experts.1 = (bf16[256,2048]{1,0:T(8,128)(2,1)}, bf16[4,1024,640]{2,1,0:T(8,128)(2,1)}, bf16[4,1024,640]{2,1,0:T(8,128)(2,1)}, bf16[4,1024,768]{2,1,0:T(8,128)(2...) custom-call(bf16[4,4,4,2,32,2048]{5,4,3,2,1,0:T(8,128)(2,1)} %get-tuple-el, ...), custom_call_target="tpu_custom_call" | custom-call | tf_op jit(solution)/shard_map/experts/pallas_call | solution.py:549
  350.2 2.3 copy.43
  (10 shorter events, 0.1 us)
